TPU v7x, 256 devices: a whole 4x4x8 slice. The times are simulated.
256 devices in a mesh: gx: 16 (over x, y_lo, core), gy: 16 (over y_hi, z).
Axes of the slice: x: 4, y: 4 (y_hi: 2, y_lo: 2; y = y_hi * 2 + y_lo), z: 8, core: 2. Of those that a mesh axis runs over, the one named last changes fastest.
Arguments:
- spectrum: float32 [384, 640, 1080], P('gx', 'gy'), may hold values from 0.05 to 1
- adjoint_in: float32 [384, 640, 1080], P('gx', 'gy'), may hold values from 0 to 2
- current_x: float32 [384, 640], P('gx', 'gy'), may hold values from -0.08 to 0.08
- current_y: float32 [384, 640], P('gx', 'gy'), may hold values from -0.08 to 0.08
- wind_x: float32 [384, 640], P('gx', 'gy'), may hold values from -4 to 4
- wind_y: float32 [384, 640], P('gx', 'gy'), may hold values from -4 to 4
- land_mask: int32 [384, 640], P('gx', 'gy'), may hold values from 0 to 1, as said below
- ice_mask: int32 [384, 640], P('gx', 'gy'), may hold values from 0 to 1, as said below
- group_speed: float32 [30], replicated, may hold values from 0.1 to 0.4
- growth_rate: float32 [30], replicated, may hold values from 0.1 to 1
- dissipation: float32 [30], replicated, may hold values from 0.3 to 3
Outputs:
- adjoint_spectrum: float32 [384, 640, 1080], P('gx', 'gy')
Inputs may be any that keep to these rules, and one draw needn't show every extreme that they name: `land_mask`: 1 marks land, 0 sea. `ice_mask`: 1 marks sea ice, 0 open water.
All inputs are finite; a program needn't handle non-finite values.
Results may differ from a plain program's by a relative error of at most 0.0001.
Values sent between devices are 32-bit elements; how exact they have to be, the bound alone decides.
A program may use at most 128 MiB of HBM per device.

v0:
```python
import math

import jax
import jax.numpy as jnp
from jax import lax
from jax.sharding import PartitionSpec as P

DIRS = 36


def with_halo(block, sides, width):
    for axis, dim in sides:
        count = lax.axis_size(axis)
        forward = [(i, i + 1) for i in range(count - 1)]
        forward.append((count - 1, 0))
        backward = [(target, source) for source, target in forward]
        low = lax.ppermute(
            lax.slice_in_dim(block, block.shape[dim] - width, None, axis=dim), axis, forward
        )
        high = lax.ppermute(lax.slice_in_dim(block, 0, width, axis=dim), axis, backward)
        block = jnp.concatenate([low, block, high], axis=dim)
    return block


def face_lon(statics, cosine, speeds):
    sea_mask = statics[..., 2]
    opened = sea_mask[:-1] * sea_mask[1:]
    drift_avg = 0.5 * (statics[:-1, :, 0] + statics[1:, :, 0])
    courant = opened[..., None] * (speeds * cosine + drift_avg[..., None])
    return (jnp.maximum(courant, 0.0), jnp.minimum(courant, 0.0))


def face_lat(statics, sine_bin, speeds):
    sea_mask = statics[..., 2]
    opened = sea_mask[:, :-1] * sea_mask[:, 1:]
    drift_avg = 0.5 * (statics[:, :-1, 1] + statics[:, 1:, 1])
    courant = opened[..., None] * (speeds * sine_bin + drift_avg[..., None])
    return (jnp.maximum(courant, 0.0), jnp.minimum(courant, 0.0))


def advect(lon_field, lat_field, lon_statics, lat_statics, tables):
    lon_plus, lon_minus = face_lon(lon_statics, tables[0], tables[2])
    lat_plus, lat_minus = face_lat(lat_statics, tables[1], tables[2])
    lon_flux = lon_plus * lon_field[:-1] + lon_minus * lon_field[1:]
    lat_flux = lat_plus * lat_field[:, :-1] + lat_minus * lat_field[:, 1:]
    centre = lon_field[1:-1]
    advected = centre - (lon_flux[1:] - lon_flux[:-1]) - (lat_flux[:, 1:] - lat_flux[:, :-1])
    return (advected, lon_plus, lon_minus, lat_plus, lat_minus)


def source_adjoint(advected, incoming, sea_mask, wind_east, wind_north, ice_free, tables):
    cosine, sine_bin, growth, damping = (tables[0], tables[1], tables[3], tables[4])
    project = wind_east[..., None] * cosine + wind_north[..., None] * sine_bin
    gained = 1.0 + growth * jnp.maximum(project, 0.0) * ice_free[..., None]
    energy = jnp.sum(advected, axis=2, keepdims=True) / advected.shape[2]
    damped = 1.0 + damping * energy * advected
    weighted = incoming * gained / (damped * damped)
    coupling = jnp.sum(weighted * damping * advected * advected, axis=2, keepdims=True)
    return sea_mask[..., None] * (weighted - coupling / advected.shape[2])


def body(
    spectrum,
    adjoint_in,
    current_x,
    current_y,
    wind_x,
    wind_y,
    land_mask,
    ice_mask,
    group_speed,
    growth_rate,
    dissipation,
):
    directions = DIRS
    angles = 2.0 * math.pi / directions * (jnp.arange(directions, dtype=jnp.float32) + 0.5)
    per_dir = group_speed.shape[0]
    cosine = jnp.repeat(jnp.cos(angles), per_dir)
    sine_bin = jnp.repeat(jnp.sin(angles), per_dir)
    tables = (
        cosine,
        sine_bin,
        jnp.tile(group_speed, directions),
        jnp.tile(growth_rate, directions),
        jnp.tile(dissipation, directions),
    )
    sea_mask = (1 - land_mask).astype(jnp.float32)
    ice_free = (1 - ice_mask).astype(jnp.float32)
    statics = jnp.stack([current_x, current_y, sea_mask, wind_x, wind_y, ice_free], axis=2)
    field_wrap, lam_wrap, stat_wrap = (
        with_halo(spectrum, (("gx", 0), ("gy", 1)), 2),
        with_halo(adjoint_in, (("gx", 0), ("gy", 1)), 2),
        with_halo(statics, (("gx", 0), ("gy", 1)), 2),
    )
    lat_index = lax.axis_index("gy")
    lat_count = lax.axis_size("gy")
    columns = jnp.arange(field_wrap.shape[1], dtype=jnp.int32)
    south_cut = jnp.logical_and(lat_index == 0, columns < 2)
    north_cut = jnp.logical_and(lat_index == lat_count - 1, columns >= field_wrap.shape[1] - 2)
    keep_cols = jnp.where(jnp.logical_or(south_cut, north_cut), 0.0, 1.0).astype(jnp.float32)[
        None, :, None
    ]
    field_all = field_wrap * keep_cols
    lam_all = lam_wrap * keep_cols
    stat_all = stat_wrap * keep_cols
    advected, lon_plus, lon_minus, lat_plus, lat_minus = advect(
        field_all[:, 1:-1], field_all[1:-1, :], stat_all[:, 1:-1], stat_all[1:-1, :], tables
    )
    cycle_stat = stat_all[1:-1, 1:-1]
    sensitivity = source_adjoint(
        advected,
        lam_all[1:-1, 1:-1],
        cycle_stat[..., 2],
        cycle_stat[..., 3],
        cycle_stat[..., 4],
        cycle_stat[..., 5],
        tables,
    )
    lon_sens = sensitivity[:, 1:-1]
    lat_sens = sensitivity[1:-1, :]
    lon_step = lon_sens[1:] - lon_sens[:-1]
    lat_step = lat_sens[:, 1:] - lat_sens[:, :-1]
    inner_lon_plus = lon_plus[1:-1, 1:-1]
    inner_lon_minus = lon_minus[1:-1, 1:-1]
    inner_lat_plus = lat_plus[1:-1, 1:-1]
    inner_lat_minus = lat_minus[1:-1, 1:-1]
    result = (
        lon_sens[1:-1] + inner_lon_plus[1:] * lon_step[1:] + inner_lon_minus[:-1] * lon_step[:-1]
    )
    result = (
        result
        + inner_lat_plus[:, 1:] * lat_step[:, 1:]
        + inner_lat_minus[:, :-1] * lat_step[:, :-1]
    )
    return result


def solution(mesh):
    placed = (
        P("gx", "gy", None),
        P("gx", "gy", None),
        P("gx", "gy"),
        P("gx", "gy"),
        P("gx", "gy"),
        P("gx", "gy"),
        P("gx", "gy"),
        P("gx", "gy"),
        P(),
        P(),
        P(),
    )
    return jax.shard_map(
        body, mesh=mesh, in_specs=placed, out_specs=P("gx", "gy", None), check_vma=False
    )
```

profile of v0, /device:TPU:16, one launch (start us, length us, event | category | flops | bytes accessed | tf_op | source)
XLA Modules:
  0.0 122.3 jit_solution(15506708653334070177)
XLA Ops:
  0.0 0.7 constant_dynamic-update-slice_fusion.5
  0.7 0.7 constant_dynamic-update-slice_fusion.4
  1.4 0.7 constant_dynamic-update-slice_fusion.3
  2.1 0.7 constant_dynamic-update-slice_fusion.2
  2.8 0.7 constant_dynamic-update-slice_fusion.1
  3.5 0.7 constant_dynamic-update-slice_fusion
  4.3 0.1 collective-permute-start
  4.4 3.8 %collective-permute-start.1 = (f32[2,40,6]{1,0,2:T(2,128)S(1)}, f32[2,40,6]{1,0,2:T(2,128)S(1)}, u32[]{:S(2)}, u32[]{:S(2)}) collective-permute-start(f32[2,40,6]{1,0,2:T(2,128)S(1)} %get-tuple-element.26), channel_id=1, source_target_pairs={{16,0},{32,16},{48,32},{64,48},{80,64},{96,80},{112,96},{128,112},... | collective-permute-start | bytes 5768 | tf_op jit(solution)/shard_map/ppermute | solution.py:20
  8.2 1.1 fusion.27
  9.3 0.1 collective-permute-start.8
  9.4 3.8 %collective-permute-start.9 = (f32[2,40,1080]{2,1,0:T(8,128)S(1)}, f32[2,40,1080]{2,1,0:T(8,128)S(1)}, u32[]{:S(2)}, u32[]{:S(2)}) collective-permute-start(f32[2,40,1080]{2,1,0:T(8,128)S(1)} %get-tuple-element.16), channel_id=1, source_target_pairs={{16,0},{32,16},{48,32},{64,48},{80,64},{96,80},{112,96},{128,112},... | collective-permute-start | bytes 1036808 | tf_op jit(solution)/shard_map/ppermute | solution.py:20
  13.3 1.1 fusion.26
  14.4 0.1 collective-permute-start.4
  14.6 0.1 broadcast_in_dim.29
  14.7 0.1 mul.227
  14.8 0.1 broadcast_in_dim.30
  14.9 0.1 mul.232
  15.0 0.7 tile.10
  15.7 0.1 tile.11
  15.8 0.6 fusion.30
  16.4 0.1 fusion.28
  16.5 2.0 %collective-permute-start.2 = (f32[28,2,6]{1,0,2:T(8,128)S(1)}, f32[28,2,6]{1,0,2:T(8,128)S(1)}, u32[]{:S(2)}, u32[]{:S(2)}) collective-permute-start(f32[28,2,6]{1,0,2:T(8,128)S(1)} %get-tuple-element.23), channel_id=1, source_target_pairs={{0,1},{1,2},{2,3},{3,4},{4,5},{5,6},{6,7},{7,8},{8,9},{9,10},{10,1... | collective-permute-start | bytes 4040 | tf_op jit(solution)/shard_map/ppermute | solution.py:17
  18.5 3.8 %collective-permute-start.3 = (f32[28,2,6]{1,0,2:T(8,128)S(1)}, f32[28,2,6]{1,0,2:T(8,128)S(1)}, u32[]{:S(2)}, u32[]{:S(2)}) collective-permute-start(f32[28,2,6]{1,0,2:T(8,128)S(1)} %get-tuple-element.24), channel_id=1, source_target_pairs={{1,0},{2,1},{3,2},{4,3},{5,4},{6,5},{7,6},{8,7},{9,8},{10,9},{11,1... | collective-permute-start | bytes 4040 | tf_op jit(solution)/shard_map/ppermute | solution.py:20
  22.3 5.3 %copy.35 = f32[24,40,1080]{2,0,1:T(8,128)} copy(f32[24,40,1080]{2,1,0:T(8,128)} %param.11) | data formatting | bytes 8294400 | tf_op args[0]
  27.7 2.9 %copy.29 = f32[24,40,1080]{2,0,1:T(8,128)} copy(f32[24,40,1080]{2,1,0:T(8,128)S(1)} %bitcast.31) | data formatting | bytes 8294400 | tf_op args[1]
  30.6 0.7 slice.237
  31.2 0.7 mul.221
  31.9 0.7 mul.240
  32.6 4.2 %collective-permute-start.5 = (f32[2,40,1080]{2,1,0:T(8,128)S(1)}, f32[2,40,1080]{2,1,0:T(8,128)}, u32[]{:S(2)}, u32[]{:S(2)}) collective-permute-start(f32[2,40,1080]{2,1,0:T(8,128)S(1)} %get-tuple-element.14), channel_id=1, source_target_pairs={{16,0},{32,16},{48,32},{64,48},{80,64},{96,80},{112,96},{128,112},... | collective-permute-start | bytes 1036808 | tf_op jit(solution)/shard_map/ppermute | solution.py:20
  36.8 0.1 maximum_multiply_fusion.1
  37.0 0.1 fusion.20
  37.1 0.1 slice_bitcast_fusion.4
  37.1 0.1 fusion.17
  37.2 0.1 slice_multiply_fusion.8
  37.3 0.7 copy.37
  38.0 0.7 copy.38
  38.7 0.7 copy.39
  39.4 0.7 copy.40
  40.1 0.7 copy.31
  40.8 0.7 copy.32
  41.5 0.7 copy.33
  42.1 0.1 copy.27
  42.3 0.2 copy.34
  42.5 0.2 copy.36
  42.7 1.4 %pad_maximum_fusion.6 = (f32[28,2,1080]{2,0,1:T(8,128)S(1)}, f32[28,2,1080]{2,0,1:T(8,128)S(1)}) fusion(f32[2,40,1080]{2,0,1:T(2,128)S(1)} %copy.36, f32[24,40,1080]{2,0,1:T(8,128)} %copy.35, f32[2,40,1080]{2,0,1:T(2,128)S(1)} %copy.34), kind=kLoop, calls=%fused_computation.39 | loop fusion | flops 241920 | bytes 5322240 | tf_op jit(solution)/shard_map/slice | solution.py:18
  44.1 0.1 collective-permute-start.10
  44.1 5.6 %collective-permute-start.11 = (f32[28,2,1080]{2,0,1:T(8,128)S(1)}, f32[28,2,1080]{2,0,1:T(8,128)S(1)}, u32[]{:S(2)}, u32[]{:S(2)}) collective-permute-start(f32[28,2,1080]{2,0,1:T(8,128)S(1)} %get-tuple-element.12), channel_id=1, source_target_pairs={{1,0},{2,1},{3,2},{4,3},{5,4},{6,5},{7,6},{8,7},{9,8},{10,9},{11,1... | collective-permute-start | bytes 725768 | tf_op jit(solution)/shard_map/ppermute | solution.py:20
  49.8 0.2 copy.28
  50.0 1.2 copy.30
  51.2 0.9 pad_maximum_fusion.9
  52.1 0.2 collective-permute-start.6
  52.3 5.6 %collective-permute-start.7 = (f32[28,2,1080]{2,0,1:T(8,128)}, f32[28,2,1080]{2,0,1:T(8,128)}, u32[]{:S(2)}, u32[]{:S(2)}) collective-permute-start(f32[28,2,1080]{2,0,1:T(8,128)} %get-tuple-element.10), channel_id=1, source_target_pairs={{1,0},{2,1},{3,2},{4,3},{5,4},{6,5},{7,6},{8,7},{9,8},{10,9},{11,1... | collective-permute-start | bytes 725768 | tf_op jit(solution)/shard_map/ppermute | solution.py:20
  58.0 2.8 %maximum_multiply_fusion = f32[28,44,1080]{2,0,1:T(8,128)S(1)} fusion(f32[28,2,1080]{2,0,1:T(8,128)S(1)} %collective-permute-done.11, f32[2,40,1080]{2,0,1:T(2,128)S(1)} %copy.36, f32[24,40,1080]{2,0,1:T(8,128)S(1)} %bitcast.29, f32[2,40,1080]{2,0,1:T(2,128)S(1)} %copy.34, f32[28,2,1080]{2,0,1:T(8,128)S(1)} %collective-permute-done.10, f32[44]{0:T(128)S(1)} %copy-done.11), kind=kLoop, calls=%fused_computation.1 | loop fusion | flops 6652800 | bytes 10644656 | tf_op jit(solution)/shard_map/mul | solution.py:103
  60.9 6.9 %fusion.11 = (f32[27,42,1080]{2,0,1:T(8,128)}, f32[27,42,1080]{2,0,1:T(8,128)S(1)}, f32[27,42,1080]{2,0,1:T(8,128)}) fusion(f32[27,42]{0,1:T(8,128)S(1)} %copy-done.6, f32[1080]{0:T(1024)S(1)} %copy-done.9, f32[27,42]{0,1:T(8,128)S(1)} %copy-done.5, f32[28,44,1080]{2,0,1:T(8,128)S(1)} %maximum_multiply_fusion), kind=kLoop, calls=%fused_computation.26 | loop fusion | flops 8573040 | bytes 24507792 | tf_op jit(solution)/shard_map/max | solution.py:30
  67.8 7.7 %fusion.2 = (f32[26,43,1080]{2,0,1:T(8,128)}, f32[26,43,1080]{2,0,1:T(8,128)S(1)}, f32[26,43,1080]{2,0,1:T(8,128)}) fusion(f32[26,43]{0,1:T(8,128)S(1)} %copy-done.4, f32[1080]{0:T(1024)S(1)} %copy-done.8, f32[26,43]{0,1:T(8,128)S(1)} %copy-done.3, f32[28,44,1080]{2,0,1:T(8,128)S(1)} %maximum_multiply_fusion), kind=kLoop, calls=%fused_computation.7 | loop fusion | flops 8452080 | bytes 24162064 | tf_op jit(solution)/shard_map/max | solution.py:38
  75.5 4.9 %fusion.24 = (f32[26,42]{0,1:T(8,128)}, f32[26,42,1080]{2,0,1:T(8,128)}) fusion(f32[26,43,1080]{2,0,1:T(8,128)S(1)} %get-tuple-element.31, f32[27,42,1080]{2,0,1:T(8,128)S(1)} %get-tuple-element.28, f32[28,44,1080]{2,0,1:T(8,128)S(1)} %maximum_multiply_fusion), kind=kLoop, calls=%fused_computation.71 | loop fusion | flops 5895708 | bytes 28309008 | tf_op jit(solution)/shard_map/reduce_sum | solution.py:55
  80.4 0.7 broadcast_multiply_fusion.1
  81.2 9.3 %fusion.3 = (f32[26,42]{0,1:T(8,128)S(1)}, f32[26,42,1080]{2,0,1:T(8,128)S(1)}) fusion(f32[26,42,1080]{2,0,1:T(8,128)} %get-tuple-element.8, f32[1080]{0:T(1024)} %mul.240, f32[26,42]{0,1:T(8,128)S(1)} %broadcast_multiply_fusion.1, f32[26,42]{0,1:T(8,128)} %copy.33, f32[1080]{0:T(1024)} %copy-done.7, f32[26,42]{0,1:T(8,128)} %copy.32, f32[1080]{0:T(1024)S(1)} %mul.227, ...), kind=kLoop, calls=%fused_computation.8 | loop fusion | flops 25944828 | bytes 14796408 | tf_op jit(solution)/shard_map/reduce_sum | solution.py:58
  90.5 0.6 subtract_multiply_fusion
  91.1 3.8 %slice_subtract_fusion.2 = f32[25,40,1080]{2,0,1:T(8,128)} fusion(f32[26,42,1080]{2,0,1:T(8,128)S(1)} %subtract_multiply_fusion), kind=kLoop, calls=%fused_computation.27 | loop fusion | flops 1080000 | bytes 12960000 | tf_op jit(solution)/shard_map/sub | solution.py:121
  94.9 0.6 copy-done
  95.5 2.6 %slice_subtract_fusion.3 = f32[24,41,1080]{2,0,1:T(8,128)} fusion(f32[26,42,1080]{2,0,1:T(8,128)S(1)} %subtract_multiply_fusion), kind=kLoop, calls=%fused_computation.28 | loop fusion | flops 1062720 | bytes 12752640 | tf_op jit(solution)/shard_map/sub | solution.py:122
  98.1 19.0 %fusion.12 = f32[24,40,1080]{2,0,1:T(8,128)} fusion(f32[24,41,1080]{2,0,1:T(8,128)} %slice_subtract_fusion.3, f32[26,43,1080]{2,0,1:T(8,128)} %get-tuple-element.32, f32[26,43,1080]{2,0,1:T(8,128)} %get-tuple-element.30, f32[25,40,1080]{2,0,1:T(8,128)} %slice_subtract_fusion.2, f32[27,42,1080]{2,0,1:T(8,128)} %get-tuple-element.29, ...), kind=kLoop, calls=%fused_computation.30 | loop fusion | flops 8294400 | bytes 41472000 | tf_op jit(solution)/shard_map/add | solution.py:131
  117.1 5.2 %copy.41 = f32[24,40,1080]{2,1,0:T(8,128)} copy(f32[24,40,1080]{2,0,1:T(8,128)} %fusion.12) | data formatting | bytes 8294400 | tf_op jit(solution)/shard_map/add | solution.py:131
  (58 shorter events, 0.3 us)
Async XLA Ops:
  4.3 12.1 %collective-permute-start = (f32[2,40,6]{1,0,2:T(2,128)S(1)}, f32[2,40,6]{1,0,2:T(2,128)S(1)}, u32[]{:S(2)}, u32[]{:S(2)}) collective-permute-start(f32[2,40,6]{1,0,2:T(2,128)S(1)} %get-tuple-element.25), channel_id=1, source_target_pairs={{0,16},{16,32},{32,48},{48,64},{64,80},{80,96},{96,112},{112,128},... | collective-permute-start | bytes 5768 | tf_op jit(solution)/shard_map/ppermute | solution.py:17
  4.4 23.3 %slice-start.2 = ((s8[4423680]{0:T(1024)(128)(4,1)}), s8[229376]{0:T(1024)(128)(4,1)S(1)}, s32[]{:S(2)}) async-start(s8[4423680]{0:T(1024)(128)(4,1)} %bitcast.30), calls=%async_computation.2 | async-start | bytes 458752
  4.4 12.0 %collective-permute-start.1 = (f32[2,40,6]{1,0,2:T(2,128)S(1)}, f32[2,40,6]{1,0,2:T(2,128)S(1)}, u32[]{:S(2)}, u32[]{:S(2)}) collective-permute-start(f32[2,40,6]{1,0,2:T(2,128)S(1)} %get-tuple-element.26), channel_id=1, source_target_pairs={{16,0},{32,16},{48,32},{64,48},{80,64},{96,80},{112,96},{128,112},... | collective-permute-start | bytes 5768 | tf_op jit(solution)/shard_map/ppermute | solution.py:20
  9.3 32.9 %collective-permute-start.8 = (f32[2,40,1080]{2,1,0:T(8,128)S(1)}, f32[2,40,1080]{2,1,0:T(8,128)S(1)}, u32[]{:S(2)}, u32[]{:S(2)}) collective-permute-start(f32[2,40,1080]{2,1,0:T(8,128)S(1)} %get-tuple-element.15), channel_id=1, source_target_pairs={{0,16},{16,32},{32,48},{48,64},{64,80},{80,96},{96,112},{112,128},... | collective-permute-start | bytes 1036808 | tf_op jit(solution)/shard_map/ppermute | solution.py:17
  9.4 33.0 %collective-permute-start.9 = (f32[2,40,1080]{2,1,0:T(8,128)S(1)}, f32[2,40,1080]{2,1,0:T(8,128)S(1)}, u32[]{:S(2)}, u32[]{:S(2)}) collective-permute-start(f32[2,40,1080]{2,1,0:T(8,128)S(1)} %get-tuple-element.16), channel_id=1, source_target_pairs={{16,0},{32,16},{48,32},{64,48},{80,64},{96,80},{112,96},{128,112},... | collective-permute-start | bytes 1036808 | tf_op jit(solution)/shard_map/ppermute | solution.py:20
  14.4 35.3 %collective-permute-start.4 = (f32[2,40,1080]{2,1,0:T(8,128)S(1)}, f32[2,40,1080]{2,1,0:T(8,128)S(1)}, u32[]{:S(2)}, u32[]{:S(2)}) collective-permute-start(f32[2,40,1080]{2,1,0:T(8,128)S(1)} %get-tuple-element.13), channel_id=1, source_target_pairs={{0,16},{16,32},{32,48},{48,64},{64,80},{80,96},{96,112},{112,128},... | collective-permute-start | bytes 1036808 | tf_op jit(solution)/shard_map/ppermute | solution.py:17
  15.0 1.5 %copy-start.7 = (f32[1080]{0:T(1024)}, f32[1080]{0:T(1024)S(1)}, u32[]{:S(2)}) copy-start(f32[1080]{0:T(1024)S(1)} %mul.232) | copy-start | bytes 12964
  16.5 16.1 %collective-permute-start.2 = (f32[28,2,6]{1,0,2:T(8,128)S(1)}, f32[28,2,6]{1,0,2:T(8,128)S(1)}, u32[]{:S(2)}, u32[]{:S(2)}) collective-permute-start(f32[28,2,6]{1,0,2:T(8,128)S(1)} %get-tuple-element.23), channel_id=1, source_target_pairs={{0,1},{1,2},{2,3},{3,4},{4,5},{5,6},{6,7},{7,8},{8,9},{9,10},{10,1... | collective-permute-start | bytes 4040 | tf_op jit(solution)/shard_map/ppermute | solution.py:17
  18.5 18.3 %collective-permute-start.3 = (f32[28,2,6]{1,0,2:T(8,128)S(1)}, f32[28,2,6]{1,0,2:T(8,128)S(1)}, u32[]{:S(2)}, u32[]{:S(2)}) collective-permute-start(f32[28,2,6]{1,0,2:T(8,128)S(1)} %get-tuple-element.24), channel_id=1, source_target_pairs={{1,0},{2,1},{3,2},{4,3},{5,4},{6,5},{7,6},{8,7},{9,8},{10,9},{11,1... | collective-permute-start | bytes 4040 | tf_op jit(solution)/shard_map/ppermute | solution.py:20
  22.3 14.5 %copy-start.10 = (f32[44]{0:T(128)}, f32[44]{0:T(128)S(1)}, u32[]{:S(2)}) copy-start(f32[44]{0:T(128)S(1)} %or_select_fusion) | copy-start | bytes 532
  22.3 5.4 %slice-start.3 = ((s8[4423680]{0:T(1024)(128)(4,1)}), s8[4194304]{0:T(1024)(128)(4,1)S(1)}, s32[]{:S(2)}) async-start(s8[4423680]{0:T(1024)(128)(4,1)} %bitcast.30), calls=%async_computation.3 | async-start | bytes 8388608
  27.7 3.5 %copy-start.12 = (f32[30]{0:T(128)S(1)}, f32[30]{0:T(128)}, u32[]{:S(2)}) copy-start(f32[30]{0:T(128)} %param.20) | copy-start | bytes 364
  27.7 4.3 %copy-start.13 = (f32[30]{0:T(128)S(1)}, f32[30]{0:T(128)}, u32[]{:S(2)}) copy-start(f32[30]{0:T(128)} %param.21) | copy-start | bytes 364
  32.6 17.3 %collective-permute-start.5 = (f32[2,40,1080]{2,1,0:T(8,128)S(1)}, f32[2,40,1080]{2,1,0:T(8,128)}, u32[]{:S(2)}, u32[]{:S(2)}) collective-permute-start(f32[2,40,1080]{2,1,0:T(8,128)S(1)} %get-tuple-element.14), channel_id=1, source_target_pairs={{16,0},{32,16},{48,32},{64,48},{80,64},{96,80},{112,96},{128,112},... | collective-permute-start | bytes 1036808 | tf_op jit(solution)/shard_map/ppermute | solution.py:20
  42.1 15.8 %slice-start = ((s8[4423680]{0:T(1024)(128)(4,1)}), s8[229376]{0:T(1024)(128)(4,1)S(1)}, s32[]{:S(2)}) async-start(s8[4423680]{0:T(1024)(128)(4,1)} %bitcast.28), calls=%async_computation | async-start | bytes 458752
  42.2 8.9 %copy-start.1 = (f32[24,40,1080]{2,0,1:T(8,128)S(1)}, f32[24,40,1080]{2,0,1:T(8,128)}, u32[]{:S(2)}) copy-start(f32[24,40,1080]{2,0,1:T(8,128)} %copy.29) | copy-start | bytes 12441604
  42.7 15.3 %slice-start.1 = ((s8[4423680]{0:T(1024)(128)(4,1)}), s8[4194304]{0:T(1024)(128)(4,1)S(1)}, s32[]{:S(2)}) async-start(s8[4423680]{0:T(1024)(128)(4,1)} %bitcast.28), calls=%async_computation.1 | async-start | bytes 8388608
  42.7 15.3 %copy-start.11 = (f32[44]{0:T(128)S(1)}, f32[44]{0:T(128)}, u32[]{:S(2)}) copy-start(f32[44]{0:T(128)} %copy-done.10) | copy-start | bytes 532
  44.1 13.9 %collective-permute-start.10 = (f32[28,2,1080]{2,0,1:T(8,128)S(1)}, f32[28,2,1080]{2,0,1:T(8,128)S(1)}, u32[]{:S(2)}, u32[]{:S(2)}) collective-permute-start(f32[28,2,1080]{2,0,1:T(8,128)S(1)} %get-tuple-element.11), channel_id=1, source_target_pairs={{0,1},{1,2},{2,3},{3,4},{4,5},{5,6},{6,7},{7,8},{8,9},{9,10},{10,1... | collective-permute-start | bytes 725768 | tf_op jit(solution)/shard_map/ppermute | solution.py:17
  44.1 13.8 %collective-permute-start.11 = (f32[28,2,1080]{2,0,1:T(8,128)S(1)}, f32[28,2,1080]{2,0,1:T(8,128)S(1)}, u32[]{:S(2)}, u32[]{:S(2)}) collective-permute-start(f32[28,2,1080]{2,0,1:T(8,128)S(1)} %get-tuple-element.12), channel_id=1, source_target_pairs={{1,0},{2,1},{3,2},{4,3},{5,4},{6,5},{7,6},{8,7},{9,8},{10,9},{11,1... | collective-permute-start | bytes 725768 | tf_op jit(solution)/shard_map/ppermute | solution.py:20
  51.2 9.7 %copy-start.2 = (f32[2,40,1080]{2,0,1:T(2,128)}, f32[2,40,1080]{2,0,1:T(2,128)S(1)}, u32[]{:S(2)}) copy-start(f32[2,40,1080]{2,0,1:T(2,128)S(1)} %copy.30) | copy-start | bytes 1036804
  52.1 8.7 %copy-start.5 = (f32[27,42]{0,1:T(8,128)S(1)}, f32[27,42]{0,1:T(8,128)}, u32[]{:S(2)}) copy-start(f32[27,42]{0,1:T(8,128)} %copy.37) | copy-start | bytes 13612
  52.1 8.7 %copy-start.6 = (f32[27,42]{0,1:T(8,128)S(1)}, f32[27,42]{0,1:T(8,128)}, u32[]{:S(2)}) copy-start(f32[27,42]{0,1:T(8,128)} %copy.38) | copy-start | bytes 13612
  52.1 8.7 %copy-start.9 = (f32[1080]{0:T(1024)S(1)}, f32[1080]{0:T(1024)}, u32[]{:S(2)}) copy-start(f32[1080]{0:T(1024)} %get-tuple-element.33) | copy-start | bytes 12964
  52.1 29.0 %collective-permute-start.6 = (f32[28,2,1080]{2,0,1:T(8,128)}, f32[28,2,1080]{2,0,1:T(8,128)}, u32[]{:S(2)}, u32[]{:S(2)}) collective-permute-start(f32[28,2,1080]{2,0,1:T(8,128)} %get-tuple-element.9), channel_id=1, source_target_pairs={{0,1},{1,2},{2,3},{3,4},{4,5},{5,6},{6,7},{7,8},{8,9},{9,10},{10,1... | collective-permute-start | bytes 725768 | tf_op jit(solution)/shard_map/ppermute | solution.py:17
  52.3 28.8 %collective-permute-start.7 = (f32[28,2,1080]{2,0,1:T(8,128)}, f32[28,2,1080]{2,0,1:T(8,128)}, u32[]{:S(2)}, u32[]{:S(2)}) collective-permute-start(f32[28,2,1080]{2,0,1:T(8,128)} %get-tuple-element.10), channel_id=1, source_target_pairs={{1,0},{2,1},{3,2},{4,3},{5,4},{6,5},{7,6},{8,7},{9,8},{10,9},{11,1... | collective-permute-start | bytes 725768 | tf_op jit(solution)/shard_map/ppermute | solution.py:20
  60.9 6.9 %copy-start.3 = (f32[26,43]{0,1:T(8,128)S(1)}, f32[26,43]{0,1:T(8,128)}, u32[]{:S(2)}) copy-start(f32[26,43]{0,1:T(8,128)} %copy.39) | copy-start | bytes 13420
  60.9 6.9 %copy-start.4 = (f32[26,43]{0,1:T(8,128)S(1)}, f32[26,43]{0,1:T(8,128)}, u32[]{:S(2)}) copy-start(f32[26,43]{0,1:T(8,128)} %copy.40) | copy-start | bytes 13420
  60.9 6.9 %copy-start.8 = (f32[1080]{0:T(1024)S(1)}, f32[1080]{0:T(1024)}, u32[]{:S(2)}) copy-start(f32[1080]{0:T(1024)} %get-tuple-element.34) | copy-start | bytes 12964
  91.1 4.3 %copy-start = (f32[26,42,1080]{2,0,1:T(8,128)}, f32[26,42,1080]{2,0,1:T(8,128)S(1)}, u32[]{:S(2)}) copy-start(f32[26,42,1080]{2,0,1:T(8,128)S(1)} %subtract_multiply_fusion) | copy-start | bytes 14152324
where the time goes:
time: 123 us; the launch traced here: 122 us
  other arithmetic  63.2 us (51%)
  starting transfers between devices  29.4 us (24%)
  local copies, waits for them, and re-layouts  29.2 us (24%)
    ppermute x6, starting transfers between devices, with_halo(): lax.ppermute(lax.slice_in_dim(block, 0, width, axis=dim), axis, backward)  26.9 us
    add x1, other arithmetic, body(): result + inner_lat_plus[:, 1:] * lat_step[:, 1:]  19 us
    unnamed x42, local copies, waits for them, and re-layouts  11.7 us
    reduce_sum x1, other arithmetic, source_adjoint(): jnp.sum(weighted * damping * advected * advected, axis=2, keepdims=True)  9.34 us
    max x1, other arithmetic, face_lat(): return (jnp.maximum(courant, 0.0), jnp.minimum(courant, 0.0))  7.69 us
    max x1, other arithmetic, face_lon(): return (jnp.maximum(courant, 0.0), jnp.minimum(courant, 0.0))  6.91 us
    add x1, local copies, waits for them, and re-layouts, body(): result + inner_lat_plus[:, 1:] * lat_step[:, 1:]  5.19 us
    reduce_sum x1, other arithmetic, source_adjoint(): energy = jnp.sum(advected, axis=2, keepdims=True) / advected.shape[2]  4.91 us
  transfers between devices with their start and end apart: 12, of which 0 were waited for; matrix products, arithmetic and copies ran while one was open for 38% of the time, Pallas kernels for 0%

commit v1 on v0

v1 whole, which is shorter than its diff:
```python
import math

import jax
import jax.numpy as jnp
import numpy as np
from jax import lax
from jax.experimental import pallas as pl
from jax.experimental.pallas import tpu as pltpu
from jax.sharding import PartitionSpec as P

DIRS = 36
LANES = 128
PAD = 8
MESH = pl.DeviceIdType.MESH


def kernel(
    spec_hbm,
    adj_hbm,
    cx_hbm,
    cy_hbm,
    wx_hbm,
    wy_hbm,
    land_hbm,
    ice_hbm,
    tab_hbm,
    out,
    sp_main,
    sp_tail,
    ss_main,
    ss_tail,
    inc,
    adv,
    oxs,
    pxs,
    oys,
    pys,
    wxs,
    wys,
    seas,
    tab_in,
    tab,
    stat_f,
    stat_i,
    nb_f,
    nb_i,
    ext,
    load_sem,
    send_sem,
    recv_sem,
):
    rows, cols, bins = spec_hbm.shape
    mains = bins // LANES
    tail = bins - mains * LANES
    tiles = cols // 8
    pieces = mains + 1
    gx = lax.axis_index("gx")
    gy = lax.axis_index("gy")
    nx = lax.axis_size("gx")
    ny = lax.axis_size("gy")
    east = lax.rem(gx + 1, nx)
    west = lax.rem(gx + nx - 1, nx)
    has_north = gy < ny - 1
    has_south = gy > 0
    body = pl.ds(PAD, cols)

    def local(src, dst, k):
        return pltpu.make_async_copy(src, dst, load_sem.at[k])

    def loads_of(low, count, base):
        copies = []
        for t in range(pieces):
            src_lanes = pl.ds(t * LANES, LANES if t < mains else tail)
            src = spec_hbm.at[pl.ds(low, count), :, src_lanes]
            if t < mains:
                dst = sp_main.at[pl.ds(low + 1, count), t, body, :]
            else:
                dst = sp_tail.at[pl.ds(low + 1, count), body, :]
            copies.append(local(src, dst, base + t))
        return copies

    first_row = loads_of(0, 1, 0)
    last_row = loads_of(rows - 1, 1, pieces)
    bulk = loads_of(1, rows - 2, 2 * pieces)
    base = 3 * pieces
    small = [
        local(land_hbm, stat_i.at[0], base),
        local(cx_hbm, stat_f.at[0], base + 1),
        local(cy_hbm, stat_f.at[1], base + 2),
        local(wx_hbm, stat_f.at[2], base + 3),
        local(wy_hbm, stat_f.at[3], base + 4),
        local(ice_hbm, stat_i.at[1], base + 5),
        local(tab_hbm, tab_in, base + 6),
    ]
    inc_load = local(adj_hbm, inc, base + 7)
    for copy in small + last_row + first_row + bulk + [inc_load]:
        copy.start()

    barrier = pltpu.get_barrier_semaphore()
    for target in (east, west):
        pl.semaphore_signal(barrier, inc=1, device_id={"gx": target}, device_id_type=MESH)

    @pl.when(has_north)
    def _():
        pl.semaphore_signal(barrier, inc=1, device_id={"gy": gy + 1}, device_id_type=MESH)

    @pl.when(has_south)
    def _():
        pl.semaphore_signal(barrier, inc=1, device_id={"gy": gy - 1}, device_id_type=MESH)

    def zero_line(line):
        def step(r, carry):
            for main, last in ((sp_main, sp_tail), (ss_main, ss_tail)):
                for t in range(mains):
                    main[r, t, pl.ds(line, 1), :] = jnp.zeros((1, LANES), jnp.float32)
                last[r, pl.ds(line, 1), :] = jnp.zeros((1, tail), jnp.float32)
            return carry

        lax.fori_loop(1, rows + 1, step, 0)

    @pl.when(gy == 0)
    def _():
        zero_line(PAD - 1)

    @pl.when(gy == ny - 1)
    def _():
        zero_line(PAD + cols)

    peers = 2 + lax.div(gy + ny - 1, ny) + lax.div(2 * ny - 2 - gy, ny)
    pl.semaphore_wait(barrier, peers)

    def remote(src, dst, k, device):
        return pltpu.make_async_remote_copy(
            src_ref=src,
            dst_ref=dst,
            send_sem=send_sem.at[k],
            recv_sem=recv_sem.at[k],
            device_id=device,
            device_id_type=MESH,
        )

    to_east, to_west = {"gx": east}, {"gx": west}
    to_north, to_south = {"gy": gy + 1}, {"gy": gy - 1}

    def edge(main, last, k, side):
        inner = pl.ds(1, rows)
        if side == "east":
            src, dst = (rows, body), (0, body)
            device = to_east
        elif side == "west":
            src, dst = (1, body), (rows + 1, body)
            device = to_west
        elif side == "north":
            src = (inner, pl.ds(PAD + cols - 1, 1))
            dst = (inner, pl.ds(PAD - 1, 1))
            device = to_north
        else:
            src = (inner, pl.ds(PAD, 1))
            dst = (inner, pl.ds(PAD + cols, 1))
            device = to_south
        return [
            remote(main.at[src[0], :, src[1], :], main.at[dst[0], :, dst[1], :], k, device),
            remote(last.at[src[0], src[1], :], last.at[dst[0], dst[1], :], k + 1, device),
        ]

    sides = ("east", "west", "north", "south")
    stat_copies = {}
    for s, (side, device, field) in enumerate(
        (("east", to_east, 0), ("west", to_west, 0), ("north", to_north, 1), ("south", to_south, 1))
    ):
        stat_copies[side] = [
            remote(stat_i.at[0], nb_i.at[s], 16 + 2 * s, device),
            remote(stat_f.at[field], nb_f.at[s], 17 + 2 * s, device),
        ]
    one = {side: edge(sp_main, sp_tail, 2 * s, side) for s, side in enumerate(sides)}
    two = {side: edge(ss_main, ss_tail, 8 + 2 * s, side) for s, side in enumerate(sides)}

    sends_ok = {"east": None, "west": None, "north": has_north, "south": has_south}
    recvs_ok = {"east": None, "west": None, "north": has_south, "south": has_north}

    def guarded(condition, run):
        if condition is None:
            run()
        else:
            pl.when(condition)(run)

    def start(group, side):
        guarded(sends_ok[side], lambda: [copy.start() for copy in group[side]] and None)

    def wait_recv(group, side):
        guarded(recvs_ok[side], lambda: [copy.wait_recv() for copy in group[side]] and None)

    def wait_send(group, side):
        guarded(sends_ok[side], lambda: [copy.wait_send() for copy in group[side]] and None)

    for copy in small[:3]:
        copy.wait()
    for side in sides:
        start(stat_copies, side)
    for copy in last_row:
        copy.wait()
    start(one, "east")
    for copy in first_row:
        copy.wait()
    start(one, "west")
    for copy in bulk:
        copy.wait()
    start(one, "north")
    start(one, "south")

    for copy in small[3:]:
        copy.wait()
    for k in range(5):
        for t in range(pieces):
            width = LANES if t < mains else tail
            line = tab_in[pl.ds(k, 1), pl.ds(t * LANES, width)]
            tab[k * pieces + t, :, pl.ds(0, width)] = jnp.broadcast_to(line, (8, width))

    for side in sides:
        wait_recv(stat_copies, side)

    lane = lax.broadcasted_iota(jnp.int32, (32, LANES), 1)
    row = lax.broadcasted_iota(jnp.int32, (32, LANES), 0)

    def widened(values):
        ext[...] = jnp.zeros((32, LANES), jnp.float32)
        ext[pl.ds(0, rows), pl.ds(0, cols)] = values
        return ext[...]

    def sea_of(mask):
        return (1 - mask).astype(jnp.float32)

    def around_lon(mine, from_east, from_west):
        up = pltpu.roll(widened(from_east), rows, 0)
        down = pltpu.roll(widened(from_west), 8, 0)
        return jnp.where(row == rows, up, jnp.where(row == 31, down, mine))

    def around_lat(mine, from_north, from_south):
        up = pltpu.roll(widened(from_north), cols, 1)
        down = pltpu.roll(widened(from_south), LANES - cols, 1)
        up = jnp.where(has_north, up, 0.0)
        down = jnp.where(has_south, down, 0.0)
        return jnp.where(lane == cols, up, jnp.where(lane == LANES - 1, down, mine))

    sea = widened(sea_of(stat_i[0]))
    ice_free = widened(sea_of(stat_i[1]))
    sea_lon = around_lon(sea, sea_of(nb_i[1]), sea_of(nb_i[0]))
    sea_lat = around_lat(sea, sea_of(nb_i[3]), sea_of(nb_i[2]))
    drift_lon = around_lon(widened(stat_f[0]), nb_f[1], nb_f[0])
    drift_lat = around_lat(widened(stat_f[1]), nb_f[3], nb_f[2])
    open_lon = sea_lon * pltpu.roll(sea_lon, 31, 0)
    push_lon = open_lon * (0.5 * (drift_lon + pltpu.roll(drift_lon, 31, 0)))
    open_lat = sea_lat * pltpu.roll(sea_lat, LANES - 1, 1)
    push_lat = open_lat * (0.5 * (drift_lat + pltpu.roll(drift_lat, LANES - 1, 1)))
    wet = ice_free * sea
    wind_x = widened(stat_f[2]) * wet
    wind_y = widened(stat_f[3]) * wet

    def spread(field, dst, lat_faces=False, lon_faces=False):
        turned = jnp.transpose(field)
        if lon_faces:
            order = [31] + list(range(rows))
        else:
            order = list(range(rows))
        for at, r in enumerate(order):
            column = turned[:cols, r : r + 1]
            if lat_faces:
                dst[at, pl.ds(PAD, cols), :] = jnp.broadcast_to(column, (cols, LANES))
                first = turned[LANES - 1 :, r : r + 1]
                dst[at, pl.ds(PAD - 1, 1), :] = jnp.broadcast_to(first, (1, LANES))
            else:
                dst[at, :, :] = jnp.broadcast_to(column, (cols, LANES))

    spread(open_lon, oxs, lon_faces=True)
    spread(push_lon, pxs, lon_faces=True)
    spread(open_lat, oys, lat_faces=True)
    spread(push_lat, pys, lat_faces=True)
    spread(wind_x, wxs)
    spread(wind_y, wys)
    spread(sea, seas)

    def width_of(t):
        return LANES if t < mains else tail

    def at(main, last, r, t, line):
        if t < mains:
            return main[r, t, pl.ds(line, 8), :]
        return last[r, pl.ds(line, 8), :]

    def put(main, last, r, t, line, value):
        if t < mains:
            main[r, t, pl.ds(line, 8), :] = value
        else:
            last[r, pl.ds(line, 8), :] = value

    def table(k, t):
        return tab[k * pieces + t, :, pl.ds(0, width_of(t))]

    def faces(i, jt, t):
        cut = (slice(None), slice(0, width_of(t)))
        line = PAD + 8 * jt
        cos_speed, sin_speed = table(0, t), table(1, t)
        spot = pl.ds(8 * jt, 8)
        a_e = oxs[i + 1, spot, :][cut] * cos_speed + pxs[i + 1, spot, :][cut]
        a_w = oxs[i, spot, :][cut] * cos_speed + pxs[i, spot, :][cut]
        a_n = oys[i, pl.ds(line, 8), :][cut] * sin_speed + pys[i, pl.ds(line, 8), :][cut]
        a_s = oys[i, pl.ds(line - 1, 8), :][cut] * sin_speed + pys[i, pl.ds(line - 1, 8), :][cut]
        return a_e, a_w, a_n, a_s

    def around(main, last, i, jt, t):
        line = PAD + 8 * jt
        return (
            at(main, last, i + 1, t, line),
            at(main, last, i + 2, t, line),
            at(main, last, i, t, line),
            at(main, last, i + 1, t, line + 1),
            at(main, last, i + 1, t, line - 1),
        )

    def lane_sum(parts):
        whole = parts[0]
        for part in parts[1:mains]:
            whole = whole + part
        return jnp.sum(whole, axis=1, keepdims=True) + jnp.sum(parts[mains], axis=1, keepdims=True)

    scale = 1.0 / bins

    def source(cells):
        energies = []
        for u, (i, jt) in enumerate(cells):
            parts = []
            for t in range(pieces):
                a_e, a_w, a_n, a_s = faces(i, jt, t)
                here, e, w, n, s = around(sp_main, sp_tail, i, jt, t)
                lon = a_e * jnp.where(a_e > 0.0, here, e) - a_w * jnp.where(a_w > 0.0, w, here)
                lat = a_n * jnp.where(a_n > 0.0, here, n) - a_s * jnp.where(a_s > 0.0, s, here)
                moved = here - lon - lat
                adv[u, t, :, pl.ds(0, width_of(t))] = moved
                parts.append(moved)
            energies.append(lane_sum(parts) * scale)
        pulls = []
        for u, (i, jt) in enumerate(cells):
            parts = []
            spot = pl.ds(8 * jt, 8)
            energy = jnp.broadcast_to(energies[u], (8, LANES))
            for t in range(pieces):
                width = width_of(t)
                cut = (slice(None), slice(0, width))
                moved = adv[u, t, :, pl.ds(0, width)]
                blow = wxs[i, spot, :][cut] * table(2, t) + wys[i, spot, :][cut] * table(3, t)
                gain = jnp.maximum(blow, 0.0) + seas[i, spot, :][cut]
                loss = table(4, t) * moved
                damp = 1.0 + energy[cut] * loss
                square = damp * damp
                inverse = pl.reciprocal(square, approx=True)
                inverse = inverse * (2.0 - square * inverse)
                weighted = inc[i, spot, pl.ds(t * LANES, width)] * gain * inverse
                put(ss_main, ss_tail, i + 1, t, PAD + 8 * jt, weighted)
                parts.append(weighted * loss * moved)
            pulls.append(lane_sum(parts) * scale)
        for u, (i, jt) in enumerate(cells):
            pull = jnp.broadcast_to(pulls[u], (8, LANES))
            line = PAD + 8 * jt
            for t in range(pieces):
                value = at(ss_main, ss_tail, i + 1, t, line) - pull[:, : width_of(t)]
                put(ss_main, ss_tail, i + 1, t, line, value)

    def transport(cells):
        for i, jt in cells:
            for t in range(pieces):
                a_e, a_w, a_n, a_s = faces(i, jt, t)
                here, e, w, n, s = around(ss_main, ss_tail, i, jt, t)
                lon = jnp.maximum(a_e, 0.0) * (e - here) + jnp.minimum(a_w, 0.0) * (here - w)
                lat = jnp.maximum(a_n, 0.0) * (n - here) + jnp.minimum(a_s, 0.0) * (here - s)
                out[i, pl.ds(8 * jt, 8), pl.ds(t * LANES, width_of(t))] = here + lon + lat

    def looped(low, high, run):
        def step(i, carry):
            run(i)
            return carry

        lax.fori_loop(low, high, step, 0)

    inc_load.wait()
    middle = range(1, tiles - 1)
    looped(1, rows - 1, lambda i: source([(i, jt) for jt in middle]))
    wait_recv(one, "west")
    wait_recv(one, "east")
    wait_recv(one, "north")
    wait_recv(one, "south")
    source([(rows - 1, jt) for jt in range(tiles)])
    start(two, "east")
    source([(0, jt) for jt in range(tiles)])
    start(two, "west")
    looped(1, rows - 1, lambda i: source([(i, 0), (i, tiles - 1)]))
    start(two, "north")
    start(two, "south")
    looped(1, rows - 1, lambda i: transport([(i, jt) for jt in middle]))
    for side in sides:
        wait_recv(two, side)
    looped(1, rows - 1, lambda i: transport([(i, 0), (i, tiles - 1)]))
    transport([(0, jt) for jt in range(tiles)])
    transport([(rows - 1, jt) for jt in range(tiles)])
    for group in (stat_copies, one, two):
        for side in sides:
            wait_send(group, side)


def body(
    spectrum,
    adjoint_in,
    current_x,
    current_y,
    wind_x,
    wind_y,
    land_mask,
    ice_mask,
    group_speed,
    growth_rate,
    dissipation,
):
    rows, cols, bins = spectrum.shape
    per_dir = bins // DIRS
    angles = np.float32(2.0 * math.pi / DIRS) * (np.arange(DIRS, dtype=np.float32) + np.float32(0.5))
    cosine = jnp.asarray(np.repeat(np.cos(angles), per_dir))
    sine = jnp.asarray(np.repeat(np.sin(angles), per_dir))
    speed = jnp.tile(group_speed, DIRS)
    growth = jnp.tile(growth_rate, DIRS)
    loss = jnp.tile(dissipation, DIRS)
    zero = jnp.zeros_like(loss)
    tables = jnp.stack(
        [speed * cosine, speed * sine, growth * cosine, growth * sine, loss, zero, zero, zero]
    )
    mains = bins // LANES
    tail = bins - mains * LANES
    tall = cols + 2 * PAD
    f32 = jnp.float32
    any_space = pl.BlockSpec(memory_space=pl.ANY)
    return pl.pallas_call(
        kernel,
        out_shape=jax.ShapeDtypeStruct((rows, cols, bins), f32),
        in_specs=[any_space] * 9,
        out_specs=pl.BlockSpec(memory_space=pltpu.VMEM),
        scratch_shapes=[
            pltpu.VMEM((rows + 2, mains, tall, LANES), f32),
            pltpu.VMEM((rows + 2, tall, tail), f32),
            pltpu.VMEM((rows + 2, mains, tall, LANES), f32),
            pltpu.VMEM((rows + 2, tall, tail), f32),
            pltpu.VMEM((rows, cols, bins), f32),
            pltpu.VMEM((cols // 8, mains + 1, 8, LANES), f32),
            pltpu.VMEM((rows + 1, cols, LANES), f32),
            pltpu.VMEM((rows + 1, cols, LANES), f32),
            pltpu.VMEM((rows, tall, LANES), f32),
            pltpu.VMEM((rows, tall, LANES), f32),
            pltpu.VMEM((rows, cols, LANES), f32),
            pltpu.VMEM((rows, cols, LANES), f32),
            pltpu.VMEM((rows, cols, LANES), f32),
            pltpu.VMEM((8, bins), f32),
            pltpu.VMEM((5 * (mains + 1), 8, LANES), f32),
            pltpu.VMEM((4, rows, cols), f32),
            pltpu.VMEM((2, rows, cols), jnp.int32),
            pltpu.VMEM((4, rows, cols), f32),
            pltpu.VMEM((4, rows, cols), jnp.int32),
            pltpu.VMEM((32, LANES), f32),
            pltpu.SemaphoreType.DMA((3 * (mains + 1) + 8,)),
            pltpu.SemaphoreType.DMA((24,)),
            pltpu.SemaphoreType.DMA((24,)),
        ],
        compiler_params=pltpu.CompilerParams(
            collective_id=0, has_side_effects=True, vmem_limit_bytes=56 * 1024 * 1024
        ),
    )(
        spectrum,
        adjoint_in,
        current_x,
        current_y,
        wind_x,
        wind_y,
        land_mask,
        ice_mask,
        tables,
    )


def solution(mesh):
    cells = P("gx", "gy", None)
    placed = (cells, cells) + (P("gx", "gy"),) * 6 + (P(),) * 3
    return jax.shard_map(body, mesh=mesh, in_specs=placed, out_specs=cells, check_vma=False)
```

time: 123 us -> 45 us (0.37)
  the two profiles are of different devices: /device:TPU:16 before, /device:TPU:24 now
where the time goes in v1:
time: 45 us; the launch traced here: 44.8 us
  Pallas kernels  37.5 us (83%)
  local copies, waits for them, and re-layouts  6.53 us (15%)
  other arithmetic  0.79 us (2%)
    pallas_call x1, Pallas kernels, body(): pl.pallas_call(kernel, out_shape=jax.ShapeDtypeStruct((rows, cols, bins),...  37.5 us
    unnamed x1, local copies, waits for them, and re-layouts  4.63 us
    another operation x8, local copies, waits for them, and re-layouts, body(): jnp.stack([speed * cosine, speed * sine, growth * cosine, growth * sine,...  1.24 us

profile of v1, /device:TPU:24, one launch (start us, length us, event | category | flops | bytes accessed | tf_op | source)
XLA Modules:
  0.0 44.8 jit_solution(13929304200191087151)
XLA Ops:
  0.0 0.7 %tile.28 = f32[36,30]{1,0:T(8,128)S(1)} broadcast(f32[30]{0:T(128)} %param.23), dimensions={1} | broadcast | bytes 4440 | tf_op jit(solution)/shard_map/tile | solution.py:429
  0.7 0.1 stack_tile.3
  0.8 0.8 %broadcast_multiply_fusion = (f32[36,30]{1,0:T(8,128)S(1)}, f32[36,30]{1,0:T(8,128)S(1)}, f32[36,30]{1,0:T(8,128)S(1)}, f32[36,30]{1,0:T(8,128)S(1)}) fusion(f32[36,30]{1,0:T(8,128)} %constant.17, f32[30]{0:T(128)} %param.22, f32[30]{0:T(128)} %param.21, f32[36,30]{1,0:T(8,128)} %constant.18), kind=kLoop, calls=%fused_computation | loop fusion | flops 4320 | bytes 26160 | tf_op jit(solution)/shard_map/mul | solution.py:432
  1.6 0.1 stack.20
  1.7 0.1 stack.18
  1.8 0.1 stack.19
  1.9 0.1 stack.21
  2.0 0.7 %stack.23.tab_hbm = f32[8,1080]{1,0:T(8,128)} concatenate(f32[1,1080]{1,0:T(1,128)S(1)} %stack.18, f32[1,1080]{1,0:T(1,128)S(1)} %stack.19, f32[1,1080]{1,0:T(1,128)S(1)} %stack.20, f32[1,1080]{1,0:T(1,128)S(1)} %stack.21, f32[1,1080]{1,0:T(1,128)S(1)} %stack_tile.3, f32[1,1080]{1,0:T(1,128)S(1)} %stack_broadcast_in_dim.3, f32[2,1080]{1,0:T(2,128)S(1)} %stack.22), dimensions={0} | concatenate | bytes 69120 | tf_op jit(solution)/shard_map/stack | solution.py:431
  2.7 37.5 %shard_map.127 = f32[24,40,1080]{2,1,0:T(8,128)} custom-call(f32[24,40,1080]{2,1,0:T(8,128)} %spec_hbm.1, f32[24,40,1080]{2,1,0:T(8,128)} %adj_hbm.1, f32[24,40]{1,0:T(8,128)} %cx_hbm.1, f32[24,40]{1,0:T(8,128)} %cy_hbm.1, f32[24,40]{1,0:T(8,128)} %wx_hbm.1, f32[24,40]{1,0:T(8,128)} %wy_hbm.1, s32[24,40]{1,0:T(8,128)} %land_hbm.1, s32[24,40]{1,0:T(8,128)} %ice_hbm.1, ...), custom_call_target="tpu_custom_call" | custom-call | tf_op jit(solution)/shard_map/pallas_call | solution.py:439
  40.2 4.6 %copy.15 = f32[24,40,1080]{2,1,0:T(8,128)} copy(f32[24,40,1080]{2,1,0:T(8,128)} %shard_map.127) | data formatting | bytes 8294400
  (2 shorter events, 0.0 us)

commit v2 on v1

--- a/solution.py
+++ b/solution.py
@@ -23,7 +23,10 @@
     wy_hbm,
     land_hbm,
     ice_hbm,
-    tab_hbm,
+    speed_hbm,
+    growth_hbm,
+    loss_hbm,
+    wave_hbm,
     out,
     sp_main,
     sp_tail,
@@ -38,7 +41,12 @@
     wxs,
     wys,
     seas,
-    tab_in,
+    fx,
+    part,
+    level,
+    par_in,
+    wave,
+    par,
     tab,
     stat_f,
     stat_i,
@@ -90,9 +98,12 @@
         local(wx_hbm, stat_f.at[2], base + 3),
         local(wy_hbm, stat_f.at[3], base + 4),
         local(ice_hbm, stat_i.at[1], base + 5),
-        local(tab_hbm, tab_in, base + 6),
+        local(speed_hbm, par_in.at[0], base + 6),
+        local(growth_hbm, par_in.at[1], base + 7),
+        local(loss_hbm, par_in.at[2], base + 8),
+        local(wave_hbm, wave, base + 9),
     ]
-    inc_load = local(adj_hbm, inc, base + 7)
+    inc_load = local(adj_hbm, inc, base + 10)
     for copy in small + last_row + first_row + bulk + [inc_load]:
         copy.start()
 
@@ -125,9 +136,6 @@
     @pl.when(gy == ny - 1)
     def _():
         zero_line(PAD + cols)
-
-    peers = 2 + lax.div(gy + ny - 1, ny) + lax.div(2 * ny - 2 - gy, ny)
-    pl.semaphore_wait(barrier, peers)
 
     def remote(src, dst, k, device):
         return pltpu.make_async_remote_copy(
@@ -193,32 +201,6 @@
     def wait_send(group, side):
         guarded(sends_ok[side], lambda: [copy.wait_send() for copy in group[side]] and None)
 
-    for copy in small[:3]:
-        copy.wait()
-    for side in sides:
-        start(stat_copies, side)
-    for copy in last_row:
-        copy.wait()
-    start(one, "east")
-    for copy in first_row:
-        copy.wait()
-    start(one, "west")
-    for copy in bulk:
-        copy.wait()
-    start(one, "north")
-    start(one, "south")
-
-    for copy in small[3:]:
-        copy.wait()
-    for k in range(5):
-        for t in range(pieces):
-            width = LANES if t < mains else tail
-            line = tab_in[pl.ds(k, 1), pl.ds(t * LANES, width)]
-            tab[k * pieces + t, :, pl.ds(0, width)] = jnp.broadcast_to(line, (8, width))
-
-    for side in sides:
-        wait_recv(stat_copies, side)
-
     lane = lax.broadcasted_iota(jnp.int32, (32, LANES), 1)
     row = lax.broadcasted_iota(jnp.int32, (32, LANES), 0)
 
@@ -242,42 +224,71 @@
         down = jnp.where(has_south, down, 0.0)
         return jnp.where(lane == cols, up, jnp.where(lane == LANES - 1, down, mine))
 
-    sea = widened(sea_of(stat_i[0]))
-    ice_free = widened(sea_of(stat_i[1]))
-    sea_lon = around_lon(sea, sea_of(nb_i[1]), sea_of(nb_i[0]))
-    sea_lat = around_lat(sea, sea_of(nb_i[3]), sea_of(nb_i[2]))
-    drift_lon = around_lon(widened(stat_f[0]), nb_f[1], nb_f[0])
-    drift_lat = around_lat(widened(stat_f[1]), nb_f[3], nb_f[2])
-    open_lon = sea_lon * pltpu.roll(sea_lon, 31, 0)
-    push_lon = open_lon * (0.5 * (drift_lon + pltpu.roll(drift_lon, 31, 0)))
-    open_lat = sea_lat * pltpu.roll(sea_lat, LANES - 1, 1)
-    push_lat = open_lat * (0.5 * (drift_lat + pltpu.roll(drift_lat, LANES - 1, 1)))
-    wet = ice_free * sea
-    wind_x = widened(stat_f[2]) * wet
-    wind_y = widened(stat_f[3]) * wet
-
-    def spread(field, dst, lat_faces=False, lon_faces=False):
+    def spread(field, places):
         turned = jnp.transpose(field)
-        if lon_faces:
-            order = [31] + list(range(rows))
-        else:
-            order = list(range(rows))
-        for at, r in enumerate(order):
-            column = turned[:cols, r : r + 1]
-            if lat_faces:
-                dst[at, pl.ds(PAD, cols), :] = jnp.broadcast_to(column, (cols, LANES))
-                first = turned[LANES - 1 :, r : r + 1]
-                dst[at, pl.ds(PAD - 1, 1), :] = jnp.broadcast_to(first, (1, LANES))
-            else:
-                dst[at, :, :] = jnp.broadcast_to(column, (cols, LANES))
-
-    spread(open_lon, oxs, lon_faces=True)
-    spread(push_lon, pxs, lon_faces=True)
-    spread(open_lat, oys, lat_faces=True)
-    spread(push_lat, pys, lat_faces=True)
-    spread(wind_x, wxs)
-    spread(wind_y, wys)
-    spread(sea, seas)
+        for dst, spot, column, r in places:
+            count = column.stop - column.start
+            dst[spot] = jnp.broadcast_to(turned[column, r : r + 1], (count, LANES))
+
+    inside = slice(0, cols)
+    inside_at = pl.ds(PAD, cols)
+
+    def lon_faces(sea_lon, drift_lon):
+        opened = sea_lon * pltpu.roll(sea_lon, 31, 0)
+        return opened, opened * (0.5 * (drift_lon + pltpu.roll(drift_lon, 31, 0)))
+
+    def lat_faces(sea_lat, drift_lat):
+        opened = sea_lat * pltpu.roll(sea_lat, LANES - 1, 1)
+        return opened, opened * (0.5 * (drift_lat + pltpu.roll(drift_lat, LANES - 1, 1)))
+
+    def prepare():
+        for copy in small[3:]:
+            copy.wait()
+        par[...] = jnp.zeros((8, LANES), jnp.float32)
+        freqs = speed_hbm.shape[1]
+        for k in range(3):
+            par[pl.ds(k, 1), pl.ds(0, freqs)] = par_in[k]
+        per_freq = par[...]
+        bin_lane = lax.broadcasted_iota(jnp.int32, (8, LANES), 1)
+        for t in range(pieces):
+            freq = lax.rem(bin_lane + t * LANES, freqs)
+            picked = jnp.take_along_axis(per_freq, freq, axis=1)
+            full = (8, LANES)
+            speed = jnp.broadcast_to(picked[0:1], full)
+            growth = jnp.broadcast_to(picked[1:2], full)
+            cosine = jnp.broadcast_to(wave[pl.ds(0, 1), pl.ds(t * LANES, LANES)], full)
+            sine = jnp.broadcast_to(wave[pl.ds(1, 1), pl.ds(t * LANES, LANES)], full)
+            tab[t] = speed * cosine
+            tab[pieces + t] = speed * sine
+            tab[2 * pieces + t] = growth * cosine
+            tab[3 * pieces + t] = growth * sine
+            tab[4 * pieces + t] = jnp.broadcast_to(picked[2:3], full)
+        sea = widened(sea_of(stat_i[0]))
+        wet = widened(sea_of(stat_i[1])) * sea
+        every = range(rows)
+        spread(sea, [(seas, r, inside, r) for r in every])
+        spread(widened(stat_f[2]) * wet, [(wxs, r, inside, r) for r in every])
+        spread(widened(stat_f[3]) * wet, [(wys, r, inside, r) for r in every])
+        for field, dst in zip(lon_faces(sea, widened(stat_f[0])), (oxs, pxs)):
+            spread(field, [(dst, r + 1, inside, r) for r in range(rows - 1)])
+        for field, dst in zip(lat_faces(sea, widened(stat_f[1])), (oys, pys)):
+            spread(field, [(dst, (r, inside_at), inside, r) for r in every])
+
+    def prepare_edges():
+        sea = widened(sea_of(stat_i[0]))
+        sea_lon = around_lon(sea, sea_of(nb_i[1]), sea_of(nb_i[0]))
+        sea_lat = around_lat(sea, sea_of(nb_i[3]), sea_of(nb_i[2]))
+        drift_lon = around_lon(widened(stat_f[0]), nb_f[1], nb_f[0])
+        drift_lat = around_lat(widened(stat_f[1]), nb_f[3], nb_f[2])
+        for field, dst in zip(lon_faces(sea_lon, drift_lon), (oxs, pxs)):
+            spread(field, [(dst, 0, inside, 31), (dst, rows, inside, rows - 1)])
+        last, before = slice(cols - 1, cols), slice(LANES - 1, LANES)
+        for field, dst in zip(lat_faces(sea_lat, drift_lat), (oys, pys)):
+            spread(
+                field,
+                [(dst, (r, pl.ds(PAD - 1, 1)), before, r) for r in range(rows)]
+                + [(dst, (r, pl.ds(PAD + cols - 1, 1)), last, r) for r in range(rows)],
+            )
 
     def width_of(t):
         return LANES if t < mains else tail
@@ -317,36 +328,67 @@
             at(main, last, i + 1, t, line - 1),
         )
 
-    def lane_sum(parts):
+    scale = 1.0 / bins
+
+    def lon_flux(i, jt, t):
+        cut = (slice(None), slice(0, width_of(t)))
+        spot = pl.ds(8 * jt, 8)
+        line = PAD + 8 * jt
+        pace = oxs[i + 1, spot, :][cut] * table(0, t) + pxs[i + 1, spot, :][cut]
+        here, e = at(sp_main, sp_tail, i + 1, t, line), at(sp_main, sp_tail, i + 2, t, line)
+        return pace * jnp.where(pace > 0.0, here, e)
+
+    def tally(i, jt, parts):
         whole = parts[0]
-        for part in parts[1:mains]:
-            whole = whole + part
-        return jnp.sum(whole, axis=1, keepdims=True) + jnp.sum(parts[mains], axis=1, keepdims=True)
-
-    scale = 1.0 / bins
-
-    def source(cells):
-        energies = []
-        for u, (i, jt) in enumerate(cells):
+        for more in parts[1:mains]:
+            whole = whole + more
+        part[i, jt] = whole
+        part[i, jt, :, pl.ds(0, tail)] = whole[:, :tail] + parts[mains]
+
+    def prime(i, jts):
+        for jt in jts:
+            for t in range(pieces):
+                fx[jt, t, :, pl.ds(0, width_of(t))] = lon_flux(i - 1, jt, t)
+
+    def advect(i, jts):
+        for jt in jts:
             parts = []
-            for t in range(pieces):
-                a_e, a_w, a_n, a_s = faces(i, jt, t)
-                here, e, w, n, s = around(sp_main, sp_tail, i, jt, t)
-                lon = a_e * jnp.where(a_e > 0.0, here, e) - a_w * jnp.where(a_w > 0.0, w, here)
-                lat = a_n * jnp.where(a_n > 0.0, here, n) - a_s * jnp.where(a_s > 0.0, s, here)
-                moved = here - lon - lat
-                adv[u, t, :, pl.ds(0, width_of(t))] = moved
-                parts.append(moved)
-            energies.append(lane_sum(parts) * scale)
-        pulls = []
-        for u, (i, jt) in enumerate(cells):
-            parts = []
-            spot = pl.ds(8 * jt, 8)
-            energy = jnp.broadcast_to(energies[u], (8, LANES))
+            spot = pl.ds(PAD + 8 * jt, 8)
+            under = pl.ds(PAD + 8 * jt - 1, 8)
             for t in range(pieces):
                 width = width_of(t)
                 cut = (slice(None), slice(0, width))
-                moved = adv[u, t, :, pl.ds(0, width)]
+                sin_speed = table(1, t)
+                a_n = oys[i, spot, :][cut] * sin_speed + pys[i, spot, :][cut]
+                a_s = oys[i, under, :][cut] * sin_speed + pys[i, under, :][cut]
+                line = PAD + 8 * jt
+                here = at(sp_main, sp_tail, i + 1, t, line)
+                n = at(sp_main, sp_tail, i + 1, t, line + 1)
+                s = at(sp_main, sp_tail, i + 1, t, line - 1)
+                f_w = fx[jt, t, :, pl.ds(0, width)]
+                f_e = lon_flux(i, jt, t)
+                fx[jt, t, :, pl.ds(0, width)] = f_e
+                lat = a_n * jnp.where(a_n > 0.0, here, n) - a_s * jnp.where(a_s > 0.0, s, here)
+                moved = here - (f_e - f_w) - lat
+                adv[i, jt, t, :, pl.ds(0, width)] = moved
+                parts.append(moved)
+            tally(i, jt, parts)
+
+    def gather(low, count, jt, tall):
+        block = (pl.ds(low, count), pl.ds(jt, tall))
+        level[block] = jnp.broadcast_to(
+            jnp.sum(part[block], axis=3, keepdims=True) * scale, (count, tall, 8, LANES)
+        )
+
+    def weigh(i, jts):
+        for jt in jts:
+            parts = []
+            spot = pl.ds(8 * jt, 8)
+            energy = level[i, jt]
+            for t in range(pieces):
+                width = width_of(t)
+                cut = (slice(None), slice(0, width))
+                moved = adv[i, jt, t, :, pl.ds(0, width)]
                 blow = wxs[i, spot, :][cut] * table(2, t) + wys[i, spot, :][cut] * table(3, t)
                 gain = jnp.maximum(blow, 0.0) + seas[i, spot, :][cut]
                 loss = table(4, t) * moved
@@ -357,13 +399,28 @@
                 weighted = inc[i, spot, pl.ds(t * LANES, width)] * gain * inverse
                 put(ss_main, ss_tail, i + 1, t, PAD + 8 * jt, weighted)
                 parts.append(weighted * loss * moved)
-            pulls.append(lane_sum(parts) * scale)
-        for u, (i, jt) in enumerate(cells):
-            pull = jnp.broadcast_to(pulls[u], (8, LANES))
+            tally(i, jt, parts)
+
+    def settle(i, jts):
+        for jt in jts:
             line = PAD + 8 * jt
+            pull = level[i, jt]
             for t in range(pieces):
                 value = at(ss_main, ss_tail, i + 1, t, line) - pull[:, : width_of(t)]
                 put(ss_main, ss_tail, i + 1, t, line, value)
+
+    def source(low, count, jts):
+        jts = list(jts)
+        prime(low, jts)
+        spans = [(jts[0], len(jts))] if jts[-1] - jts[0] == len(jts) - 1 else [(jt, 1) for jt in jts]
+        for step in (advect, weigh, settle):
+            if count == 1:
+                step(low, jts)
+            else:
+                looped(low, low + count, lambda i: step(i, jts))
+            if step is not settle:
+                for jt, tall in spans:
+                    gather(low, count, jt, tall)
 
     def transport(cells):
         for i, jt in cells:
@@ -381,26 +438,59 @@
 
         lax.fori_loop(low, high, step, 0)
 
-    inc_load.wait()
     middle = range(1, tiles - 1)
-    looped(1, rows - 1, lambda i: source([(i, jt) for jt in middle]))
-    wait_recv(one, "west")
-    wait_recv(one, "east")
-    wait_recv(one, "north")
-    wait_recv(one, "south")
-    source([(rows - 1, jt) for jt in range(tiles)])
+    everywhere = range(tiles)
+    early = gy == ny // 2
+
+    def inner_source():
+        for copy in bulk:
+            copy.wait()
+        inc_load.wait()
+        prepare()
+        source(1, rows - 2, middle)
+
+    for copy in small[:3] + last_row + first_row:
+        copy.wait()
+    pl.when(early)(inner_source)
+    peers = 2 + lax.div(gy + ny - 1, ny) + lax.div(2 * ny - 2 - gy, ny)
+    pl.semaphore_wait(barrier, peers)
+    for side in sides:
+        start(stat_copies, side)
+    start(one, "east")
+    start(one, "west")
+
+    @pl.when(gy != ny // 2)
+    def _():
+        for copy in bulk:
+            copy.wait()
+
+    start(one, "north")
+    start(one, "south")
+
+    @pl.when(gy != ny // 2)
+    def _():
+        inc_load.wait()
+        prepare()
+        source(1, rows - 2, middle)
+
+    for side in sides:
+        wait_recv(stat_copies, side)
+    prepare_edges()
+    for side in sides:
+        wait_recv(one, side)
+    source(rows - 1, 1, everywhere)
     start(two, "east")
-    source([(0, jt) for jt in range(tiles)])
+    source(0, 1, everywhere)
     start(two, "west")
-    looped(1, rows - 1, lambda i: source([(i, 0), (i, tiles - 1)]))
+    source(1, rows - 2, (0, tiles - 1))
     start(two, "north")
     start(two, "south")
     looped(1, rows - 1, lambda i: transport([(i, jt) for jt in middle]))
     for side in sides:
         wait_recv(two, side)
     looped(1, rows - 1, lambda i: transport([(i, 0), (i, tiles - 1)]))
-    transport([(0, jt) for jt in range(tiles)])
-    transport([(rows - 1, jt) for jt in range(tiles)])
+    transport([(0, jt) for jt in everywhere])
+    transport([(rows - 1, jt) for jt in everywhere])
     for group in (stat_copies, one, two):
         for side in sides:
             wait_send(group, side)
@@ -420,17 +510,11 @@
     dissipation,
 ):
     rows, cols, bins = spectrum.shape
-    per_dir = bins // DIRS
+    freqs = group_speed.shape[0]
     angles = np.float32(2.0 * math.pi / DIRS) * (np.arange(DIRS, dtype=np.float32) + np.float32(0.5))
-    cosine = jnp.asarray(np.repeat(np.cos(angles), per_dir))
-    sine = jnp.asarray(np.repeat(np.sin(angles), per_dir))
-    speed = jnp.tile(group_speed, DIRS)
-    growth = jnp.tile(growth_rate, DIRS)
-    loss = jnp.tile(dissipation, DIRS)
-    zero = jnp.zeros_like(loss)
-    tables = jnp.stack(
-        [speed * cosine, speed * sine, growth * cosine, growth * sine, loss, zero, zero, zero]
-    )
+    wave = np.zeros((8, -(-bins // LANES) * LANES), np.float32)
+    wave[0, :bins] = np.repeat(np.cos(angles), freqs)
+    wave[1, :bins] = np.repeat(np.sin(angles), freqs)
     mains = bins // LANES
     tail = bins - mains * LANES
     tall = cols + 2 * PAD
@@ -438,8 +522,8 @@
     any_space = pl.BlockSpec(memory_space=pl.ANY)
     return pl.pallas_call(
         kernel,
-        out_shape=jax.ShapeDtypeStruct((rows, cols, bins), f32),
-        in_specs=[any_space] * 9,
+        out_shape=pltpu.VMEM((rows, cols, bins), f32),
+        in_specs=[any_space] * 12,
         out_specs=pl.BlockSpec(memory_space=pltpu.VMEM),
         scratch_shapes=[
             pltpu.VMEM((rows + 2, mains, tall, LANES), f32),
@@ -447,7 +531,7 @@
             pltpu.VMEM((rows + 2, mains, tall, LANES), f32),
             pltpu.VMEM((rows + 2, tall, tail), f32),
             pltpu.VMEM((rows, cols, bins), f32),
-            pltpu.VMEM((cols // 8, mains + 1, 8, LANES), f32),
+            pltpu.VMEM((rows, cols // 8, mains + 1, 8, LANES), f32),
             pltpu.VMEM((rows + 1, cols, LANES), f32),
             pltpu.VMEM((rows + 1, cols, LANES), f32),
             pltpu.VMEM((rows, tall, LANES), f32),
@@ -455,19 +539,24 @@
             pltpu.VMEM((rows, cols, LANES), f32),
             pltpu.VMEM((rows, cols, LANES), f32),
             pltpu.VMEM((rows, cols, LANES), f32),
-            pltpu.VMEM((8, bins), f32),
+            pltpu.VMEM((cols // 8, mains + 1, 8, LANES), f32),
+            pltpu.VMEM((rows, cols // 8, 8, LANES), f32),
+            pltpu.VMEM((rows, cols // 8, 8, LANES), f32),
+            pltpu.VMEM((3, 1, freqs), f32),
+            pltpu.VMEM(wave.shape, f32),
+            pltpu.VMEM((8, LANES), f32),
             pltpu.VMEM((5 * (mains + 1), 8, LANES), f32),
             pltpu.VMEM((4, rows, cols), f32),
             pltpu.VMEM((2, rows, cols), jnp.int32),
             pltpu.VMEM((4, rows, cols), f32),
             pltpu.VMEM((4, rows, cols), jnp.int32),
             pltpu.VMEM((32, LANES), f32),
-            pltpu.SemaphoreType.DMA((3 * (mains + 1) + 8,)),
+            pltpu.SemaphoreType.DMA((3 * (mains + 1) + 11,)),
             pltpu.SemaphoreType.DMA((24,)),
             pltpu.SemaphoreType.DMA((24,)),
         ],
         compiler_params=pltpu.CompilerParams(
-            collective_id=0, has_side_effects=True, vmem_limit_bytes=56 * 1024 * 1024
+            collective_id=0, has_side_effects=True, vmem_limit_bytes=50 * 1024 * 1024
         ),
     )(
         spectrum,
@@ -478,7 +567,10 @@
         wind_y,
         land_mask,
         ice_mask,
-        tables,
+        group_speed.reshape(1, freqs),
+        growth_rate.reshape(1, freqs),
+        dissipation.reshape(1, freqs),
+        jnp.asarray(wave),
     )
 
 

time: 45 us -> 30.4 us (0.68)
  Pallas kernels: 37.5 us -> 28.1 us
  local copies, waits for them, and re-layouts: 6.53 us -> 2.09 us
  other arithmetic: 0.79 us -> 0 us
    pallas_call x1, Pallas kernels: 37.5 us -> 28.1 us  [body(): pl.pallas_call(kernel, out_shape=pltpu.VMEM((rows, cols, bins), f32), in_...]
    unnamed x1, local copies, waits for them, and re-layouts: 4.63 us -> 2.09 us
    another operation x9 -> x0, local copies, waits for them, and re-layouts: 1.9 us -> none  [the longest x8 1.24 us: body(): jnp.stack([speed * cosine, speed * sine, growth * cosine, growth * sine,...]
    mul x1 -> x0, other arithmetic: 0.79 us -> none  [body(): growth * cosine]
where the time goes in v2:
time: 30.4 us; the launch traced here: 30.2 us
  Pallas kernels  28.1 us (92%)
  local copies, waits for them, and re-layouts  2.09 us (7%)
    pallas_call x1, Pallas kernels, body(): pl.pallas_call(kernel, out_shape=pltpu.VMEM((rows, cols, bins), f32), in_...  28.1 us
    unnamed x1, local copies, waits for them, and re-layouts  2.09 us

profile of v2, /device:TPU:24, one launch (start us, length us, event | category | flops | bytes accessed | tf_op | source)
XLA Modules:
  0.0 30.2 jit_solution(17339173791184192045)
XLA Ops:
  0.0 28.1 %shard_map.118 = f32[24,40,1080]{2,1,0:T(8,128)S(1)} custom-call(f32[24,40,1080]{2,1,0:T(8,128)} %spec_hbm.1, f32[24,40,1080]{2,1,0:T(8,128)} %adj_hbm.1, f32[24,40]{1,0:T(8,128)} %cx_hbm.1, f32[24,40]{1,0:T(8,128)} %cy_hbm.1, f32[24,40]{1,0:T(8,128)} %wx_hbm.1, f32[24,40]{1,0:T(8,128)} %wy_hbm.1, s32[24,40]{1,0:T(8,128)} %land_hbm.1, s32[24,40]{1,0:T(8,128)} %ice_hbm.1, ...), custom_call_target="tpu_custom_call" | custom-call | tf_op jit(solution)/shard_map/pallas_call | solution.py:523
  28.1 2.1 %copy.14 = f32[24,40,1080]{2,1,0:T(8,128)} copy(f32[24,40,1080]{2,1,0:T(8,128)S(1)} %shard_map.118) | data formatting | bytes 8294400

commit v3 on v2

--- a/solution.py
+++ b/solution.py
@@ -44,6 +44,10 @@
     fx,
     part,
     level,
+    col,
+    ci,
+    sc,
+    dc,
     par_in,
     wave,
     par,
@@ -104,7 +108,14 @@
         local(wave_hbm, wave, base + 9),
     ]
     inc_load = local(adj_hbm, inc, base + 10)
-    for copy in small + last_row + first_row + bulk + [inc_load]:
+    col_loads = [
+        local(spec_hbm.at[:, j, :], col.at[k], base + 10 + k)
+        for k, j in ((1, 0), (4, cols - 1), (2, 1), (3, cols - 2))
+    ]
+    ci_loads = [
+        local(adj_hbm.at[:, j, :], ci.at[k], base + 15 + k) for k, j in ((0, 0), (1, cols - 1))
+    ]
+    for copy in small + last_row + first_row + col_loads + bulk + ci_loads + [inc_load]:
         copy.start()
 
     barrier = pltpu.get_barrier_semaphore()
@@ -118,24 +129,6 @@
     @pl.when(has_south)
     def _():
         pl.semaphore_signal(barrier, inc=1, device_id={"gy": gy - 1}, device_id_type=MESH)
-
-    def zero_line(line):
-        def step(r, carry):
-            for main, last in ((sp_main, sp_tail), (ss_main, ss_tail)):
-                for t in range(mains):
-                    main[r, t, pl.ds(line, 1), :] = jnp.zeros((1, LANES), jnp.float32)
-                last[r, pl.ds(line, 1), :] = jnp.zeros((1, tail), jnp.float32)
-            return carry
-
-        lax.fori_loop(1, rows + 1, step, 0)
-
-    @pl.when(gy == 0)
-    def _():
-        zero_line(PAD - 1)
-
-    @pl.when(gy == ny - 1)
-    def _():
-        zero_line(PAD + cols)
 
     def remote(src, dst, k, device):
         return pltpu.make_async_remote_copy(
@@ -150,25 +143,15 @@
     to_east, to_west = {"gx": east}, {"gx": west}
     to_north, to_south = {"gy": gy + 1}, {"gy": gy - 1}
 
-    def edge(main, last, k, side):
-        inner = pl.ds(1, rows)
-        if side == "east":
-            src, dst = (rows, body), (0, body)
-            device = to_east
-        elif side == "west":
-            src, dst = (1, body), (rows + 1, body)
-            device = to_west
-        elif side == "north":
-            src = (inner, pl.ds(PAD + cols - 1, 1))
-            dst = (inner, pl.ds(PAD - 1, 1))
-            device = to_north
-        else:
-            src = (inner, pl.ds(PAD, 1))
-            dst = (inner, pl.ds(PAD + cols, 1))
-            device = to_south
+    def edge(main, last, lines, k, side):
+        if side == "north":
+            return [remote(lines.at[lines.shape[0] - 2], lines.at[0], k, to_north)]
+        if side == "south":
+            return [remote(lines.at[1], lines.at[lines.shape[0] - 1], k, to_south)]
+        src, dst, device = (rows, 0, to_east) if side == "east" else (1, rows + 1, to_west)
         return [
-            remote(main.at[src[0], :, src[1], :], main.at[dst[0], :, dst[1], :], k, device),
-            remote(last.at[src[0], src[1], :], last.at[dst[0], dst[1], :], k + 1, device),
+            remote(main.at[src, :, body, :], main.at[dst, :, body, :], k, device),
+            remote(last.at[src, body, :], last.at[dst, body, :], k + 1, device),
         ]
 
     sides = ("east", "west", "north", "south")
@@ -180,8 +163,8 @@
             remote(stat_i.at[0], nb_i.at[s], 16 + 2 * s, device),
             remote(stat_f.at[field], nb_f.at[s], 17 + 2 * s, device),
         ]
-    one = {side: edge(sp_main, sp_tail, 2 * s, side) for s, side in enumerate(sides)}
-    two = {side: edge(ss_main, ss_tail, 8 + 2 * s, side) for s, side in enumerate(sides)}
+    one = {side: edge(sp_main, sp_tail, col, 2 * s, side) for s, side in enumerate(sides)}
+    two = {side: edge(ss_main, ss_tail, sc, 8 + 2 * s, side) for s, side in enumerate(sides)}
 
     sends_ok = {"east": None, "west": None, "north": has_north, "south": has_south}
     recvs_ok = {"east": None, "west": None, "north": has_south, "south": has_north}
@@ -273,6 +256,8 @@
             spread(field, [(dst, r + 1, inside, r) for r in range(rows - 1)])
         for field, dst in zip(lat_faces(sea, widened(stat_f[1])), (oys, pys)):
             spread(field, [(dst, (r, inside_at), inside, r) for r in every])
+            for r in every:
+                dst[r, pl.ds(0, PAD), :] = jnp.zeros((PAD, LANES), jnp.float32)
 
     def prepare_edges():
         sea = widened(sea_of(stat_i[0]))
@@ -282,13 +267,15 @@
         drift_lat = around_lat(widened(stat_f[1]), nb_f[3], nb_f[2])
         for field, dst in zip(lon_faces(sea_lon, drift_lon), (oxs, pxs)):
             spread(field, [(dst, 0, inside, 31), (dst, rows, inside, rows - 1)])
-        last, before = slice(cols - 1, cols), slice(LANES - 1, LANES)
-        for field, dst in zip(lat_faces(sea_lat, drift_lat), (oys, pys)):
-            spread(
-                field,
-                [(dst, (r, pl.ds(PAD - 1, 1)), before, r) for r in range(rows)]
-                + [(dst, (r, pl.ds(PAD + cols - 1, 1)), last, r) for r in range(rows)],
-            )
+        wet = widened(sea_of(stat_i[1])) * sea
+        lon = lon_faces(sea_lon, drift_lon)
+        lat = lat_faces(sea_lat, drift_lat)
+        fields = list(lon) + [pltpu.roll(field, 1, 0) for field in lon]
+        fields += list(lat) + [pltpu.roll(field, 1, 1) for field in lat]
+        fields += [widened(stat_f[2]) * wet, widened(stat_f[3]) * wet, sea]
+        for k, j in enumerate((0, cols - 1)):
+            for m, field in enumerate(fields):
+                dc[k, m] = jnp.broadcast_to(field[0:rows, j : j + 1], (rows, LANES))
 
     def width_of(t):
         return LANES if t < mains else tail
@@ -317,16 +304,6 @@
         a_n = oys[i, pl.ds(line, 8), :][cut] * sin_speed + pys[i, pl.ds(line, 8), :][cut]
         a_s = oys[i, pl.ds(line - 1, 8), :][cut] * sin_speed + pys[i, pl.ds(line - 1, 8), :][cut]
         return a_e, a_w, a_n, a_s
-
-    def around(main, last, i, jt, t):
-        line = PAD + 8 * jt
-        return (
-            at(main, last, i + 1, t, line),
-            at(main, last, i + 2, t, line),
-            at(main, last, i, t, line),
-            at(main, last, i + 1, t, line + 1),
-            at(main, last, i + 1, t, line - 1),
-        )
 
     scale = 1.0 / bins
 
@@ -368,7 +345,7 @@
                 f_w = fx[jt, t, :, pl.ds(0, width)]
                 f_e = lon_flux(i, jt, t)
                 fx[jt, t, :, pl.ds(0, width)] = f_e
-                lat = a_n * jnp.where(a_n > 0.0, here, n) - a_s * jnp.where(a_s > 0.0, s, here)
+                lat = a_n * jnp.where(a_n < 0.0, n, here) - a_s * jnp.where(a_s > 0.0, s, here)
                 moved = here - (f_e - f_w) - lat
                 adv[i, jt, t, :, pl.ds(0, width)] = moved
                 parts.append(moved)
@@ -422,14 +399,138 @@
                 for jt, tall in spans:
                     gather(low, count, jt, tall)
 
-    def transport(cells):
+    row_at = lax.broadcasted_iota(jnp.int32, (rows, LANES), 0)
+
+    def line(main, last, r, t, place):
+        if t < mains:
+            return main.at[r, t, pl.ds(place, 1), :]
+        return last.at[r, pl.ds(place, 1), :]
+
+    def lanes_of(t):
+        return pl.ds(t * LANES, width_of(t))
+
+    def lane_sum(parts):
+        whole = parts[0]
+        for more in parts[1:mains]:
+            whole = whole + more
+        return jnp.sum(whole, axis=1, keepdims=True) + jnp.sum(parts[mains], axis=1, keepdims=True)
+
+    def wide_table(k, t):
+        return jnp.broadcast_to(tab[k * pieces + t, pl.ds(0, 1), pl.ds(0, width_of(t))], (rows, width_of(t)))
+
+    def edge_columns():
+        ends = (0, 1)
+        places = (PAD, PAD + cols - 1)
+        sums = [[], []]
+        for k in ends:
+            here_at, n_at, s_at = ((1, 2, 0), (4, 5, 3))[k]
+            for t in range(pieces):
+                width = width_of(t)
+                coef = [dc[k, m][:, :width] for m in range(8)]
+                cos_speed, sin_speed = wide_table(0, t), wide_table(1, t)
+                here = col[here_at, :, lanes_of(t)]
+                n, s = col[n_at, :, lanes_of(t)], col[s_at, :, lanes_of(t)]
+                e_end = line(sp_main, sp_tail, rows + 1, t, places[k])[...]
+                w_end = line(sp_main, sp_tail, 0, t, places[k])[...]
+                at_row = row_at[:, :width]
+                e = jnp.where(at_row == rows - 1, e_end, pltpu.roll(here, rows - 1, 0))
+                w = jnp.where(at_row == 0, w_end, pltpu.roll(here, 1, 0))
+                a_e = coef[0] * cos_speed + coef[1]
+                a_w = coef[2] * cos_speed + coef[3]
+                a_n = coef[4] * sin_speed + coef[5]
+                a_s = coef[6] * sin_speed + coef[7]
+                lon = a_e * jnp.where(a_e < 0.0, e, here) - a_w * jnp.where(a_w > 0.0, w, here)
+                lat = a_n * jnp.where(a_n < 0.0, n, here) - a_s * jnp.where(a_s > 0.0, s, here)
+                moved = here - lon - lat
+                sc[1 + k, :, lanes_of(t)] = moved
+                sums[k].append(moved)
+        energies = [lane_sum(sums[k]) * scale for k in ends]
+        pulls = [[], []]
+        for k in ends:
+            energy = jnp.broadcast_to(energies[k], (rows, LANES))
+            for t in range(pieces):
+                width = width_of(t)
+                wind_x, wind_y, open_sea = [dc[k, m][:, :width] for m in range(8, 11)]
+                moved = sc[1 + k, :, lanes_of(t)]
+                blow = wind_x * wide_table(2, t) + wind_y * wide_table(3, t)
+                gain = jnp.maximum(blow, 0.0) + open_sea
+                loss = wide_table(4, t) * moved
+                damp = 1.0 + energy[:, :width] * loss
+                square = damp * damp
+                inverse = pl.reciprocal(square, approx=True)
+                inverse = inverse * (2.0 - square * inverse)
+                weighted = ci[k, :, lanes_of(t)] * gain * inverse
+                sc[1 + k, :, lanes_of(t)] = weighted
+                pulls[k].append(weighted * loss * moved)
+        ends_pull = [lane_sum(pulls[k]) * scale for k in ends]
+        for k in ends:
+            pull = jnp.broadcast_to(ends_pull[k], (rows, LANES))
+            for t in range(pieces):
+                sc[1 + k, :, lanes_of(t)] = sc[1 + k, :, lanes_of(t)] - pull[:, : width_of(t)]
+
+    def insert_columns(which):
+        for i in which:
+            for k, place in enumerate((PAD, PAD + cols - 1)):
+                for t in range(pieces):
+                    target = line(ss_main, ss_tail, i + 1, t, place)
+                    target[...] = sc[1 + k, pl.ds(i, 1), lanes_of(t)]
+
+    def transport(cells, skip_e=False, skip_w=False):
         for i, jt in cells:
             for t in range(pieces):
                 a_e, a_w, a_n, a_s = faces(i, jt, t)
-                here, e, w, n, s = around(ss_main, ss_tail, i, jt, t)
-                lon = jnp.maximum(a_e, 0.0) * (e - here) + jnp.minimum(a_w, 0.0) * (here - w)
-                lat = jnp.maximum(a_n, 0.0) * (n - here) + jnp.minimum(a_s, 0.0) * (here - s)
-                out[i, pl.ds(8 * jt, 8), pl.ds(t * LANES, width_of(t))] = here + lon + lat
+                place = PAD + 8 * jt
+                here = at(ss_main, ss_tail, i + 1, t, place)
+                n = at(ss_main, ss_tail, i + 1, t, place + 1)
+                s = at(ss_main, ss_tail, i + 1, t, place - 1)
+                total = here
+                if not skip_e:
+                    e = at(ss_main, ss_tail, i + 2, t, place)
+                    total = total + jnp.maximum(a_e, 0.0) * (e - here)
+                if not skip_w:
+                    w = at(ss_main, ss_tail, i, t, place)
+                    total = total + jnp.minimum(a_w, 0.0) * (here - w)
+                if jt == tiles - 1:
+                    total = total + jnp.where(a_n > 0.0, a_n * (n - here), 0.0)
+                else:
+                    total = total + jnp.maximum(a_n, 0.0) * (n - here)
+                if jt == 0:
+                    total = total + jnp.where(a_s < 0.0, a_s * (here - s), 0.0)
+                else:
+                    total = total + jnp.minimum(a_s, 0.0) * (here - s)
+                out[i, pl.ds(8 * jt, 8), lanes_of(t)] = total
+
+    def finish_row(i):
+        for jt in range(tiles):
+            spot = pl.ds(8 * jt, 8)
+            for t in range(pieces):
+                cut = (slice(None), slice(0, width_of(t)))
+                here = at(ss_main, ss_tail, i + 1, t, PAD + 8 * jt)
+                if i == 0:
+                    a_w = oxs[0, spot, :][cut] * table(0, t) + pxs[0, spot, :][cut]
+                    term = jnp.minimum(a_w, 0.0) * (here - at(ss_main, ss_tail, 0, t, PAD + 8 * jt))
+                else:
+                    a_e = oxs[rows, spot, :][cut] * table(0, t) + pxs[rows, spot, :][cut]
+                    far = at(ss_main, ss_tail, rows + 1, t, PAD + 8 * jt)
+                    term = jnp.maximum(a_e, 0.0) * (far - here)
+                out[i, spot, lanes_of(t)] = out[i, spot, lanes_of(t)] + term
+
+    def finish_column(k):
+        for t in range(pieces):
+            width = width_of(t)
+            here = sc[1 + k, :, lanes_of(t)]
+            if k == 0:
+                a_s = dc[0, 6][:, :width] * wide_table(1, t) + dc[0, 7][:, :width]
+                term = jnp.where(a_s < 0.0, a_s * (here - sc[0, :, lanes_of(t)]), 0.0)
+            else:
+                a_n = dc[1, 4][:, :width] * wide_table(1, t) + dc[1, 5][:, :width]
+                term = jnp.where(a_n > 0.0, a_n * (sc[3, :, lanes_of(t)] - here), 0.0)
+            ci[k, :, lanes_of(t)] = term
+        place = pl.ds(0 if k == 0 else cols - 1, 1)
+        for i in range(rows):
+            for t in range(pieces):
+                term = ci[k, pl.ds(i, 1), lanes_of(t)]
+                out[i, place, lanes_of(t)] = out[i, place, lanes_of(t)] + term
 
     def looped(low, high, run):
         def step(i, carry):
@@ -438,59 +539,60 @@
 
         lax.fori_loop(low, high, step, 0)
 
-    middle = range(1, tiles - 1)
     everywhere = range(tiles)
     early = gy == ny // 2
-
-    def inner_source():
+    late = gy != ny // 2
+    first_part = (rows - 2) * 3 // 5
+
+    def first_source():
         for copy in bulk:
             copy.wait()
         inc_load.wait()
         prepare()
-        source(1, rows - 2, middle)
-
-    for copy in small[:3] + last_row + first_row:
+        source(1, first_part, everywhere)
+
+    def second_source():
+        source(1 + first_part, rows - 2 - first_part, everywhere)
+
+    for copy in small[:3] + last_row + first_row + col_loads[:2]:
         copy.wait()
-    pl.when(early)(inner_source)
+    pl.when(early)(first_source)
     peers = 2 + lax.div(gy + ny - 1, ny) + lax.div(2 * ny - 2 - gy, ny)
     pl.semaphore_wait(barrier, peers)
     for side in sides:
         start(stat_copies, side)
-    start(one, "east")
-    start(one, "west")
-
-    @pl.when(gy != ny // 2)
-    def _():
-        for copy in bulk:
-            copy.wait()
-
-    start(one, "north")
-    start(one, "south")
-
-    @pl.when(gy != ny // 2)
-    def _():
-        inc_load.wait()
-        prepare()
-        source(1, rows - 2, middle)
-
+    for side in ("north", "south", "east", "west"):
+        start(one, side)
+    pl.when(late)(first_source)
+    pl.when(early)(second_source)
+    for copy in col_loads[2:] + ci_loads:
+        copy.wait()
     for side in sides:
         wait_recv(stat_copies, side)
     prepare_edges()
     for side in sides:
         wait_recv(one, side)
-    source(rows - 1, 1, everywhere)
-    start(two, "east")
-    source(0, 1, everywhere)
-    start(two, "west")
-    source(1, rows - 2, (0, tiles - 1))
+    edge_columns()
     start(two, "north")
     start(two, "south")
-    looped(1, rows - 1, lambda i: transport([(i, jt) for jt in middle]))
-    for side in sides:
+    source(rows - 1, 1, everywhere)
+    source(0, 1, everywhere)
+    insert_columns((0, rows - 1))
+    start(two, "east")
+    start(two, "west")
+    pl.when(late)(second_source)
+    insert_columns(range(1, rows - 1))
+    looped(1, rows - 1, lambda i: transport([(i, jt) for jt in everywhere]))
+    transport([(0, jt) for jt in everywhere], skip_w=True)
+    transport([(rows - 1, jt) for jt in everywhere], skip_e=True)
+    for side in ("west", "east"):
         wait_recv(two, side)
-    looped(1, rows - 1, lambda i: transport([(i, 0), (i, tiles - 1)]))
-    transport([(0, jt) for jt in everywhere])
-    transport([(rows - 1, jt) for jt in everywhere])
+    finish_row(rows - 1)
+    finish_row(0)
+    wait_recv(two, "south")
+    finish_column(1)
+    wait_recv(two, "north")
+    finish_column(0)
     for group in (stat_copies, one, two):
         for side in sides:
             wait_send(group, side)
@@ -542,6 +644,10 @@
             pltpu.VMEM((cols // 8, mains + 1, 8, LANES), f32),
             pltpu.VMEM((rows, cols // 8, 8, LANES), f32),
             pltpu.VMEM((rows, cols // 8, 8, LANES), f32),
+            pltpu.VMEM((6, rows, bins), f32),
+            pltpu.VMEM((2, rows, bins), f32),
+            pltpu.VMEM((4, rows, bins), f32),
+            pltpu.VMEM((2, 11, rows, LANES), f32),
             pltpu.VMEM((3, 1, freqs), f32),
             pltpu.VMEM(wave.shape, f32),
             pltpu.VMEM((8, LANES), f32),
@@ -551,7 +657,7 @@
             pltpu.VMEM((4, rows, cols), f32),
             pltpu.VMEM((4, rows, cols), jnp.int32),
             pltpu.VMEM((32, LANES), f32),
-            pltpu.SemaphoreType.DMA((3 * (mains + 1) + 11,)),
+            pltpu.SemaphoreType.DMA((3 * (mains + 1) + 17,)),
             pltpu.SemaphoreType.DMA((24,)),
             pltpu.SemaphoreType.DMA((24,)),
         ],

time: 30.4 us -> 27.1 us (0.89)
  the two profiles are of different devices: /device:TPU:24 before, /device:TPU:17 now
where the time goes in v3:
time: 27.1 us; the launch traced here: 26.9 us
  Pallas kernels  24.8 us (92%)
  local copies, waits for them, and re-layouts  2.09 us (8%)
    pallas_call x1, Pallas kernels, body(): pl.pallas_call(kernel, out_shape=pltpu.VMEM((rows, cols, bins), f32), in_...  24.8 us
    unnamed x1, local copies, waits for them, and re-layouts  2.09 us

profile of v3, /device:TPU:17, one launch (start us, length us, event | category | flops | bytes accessed | tf_op | source)
XLA Modules:
  0.0 26.9 jit_solution(12724814792446371419)
XLA Ops:
  0.0 24.8 %shard_map.118 = f32[24,40,1080]{2,1,0:T(8,128)S(1)} custom-call(f32[24,40,1080]{2,1,0:T(8,128)} %spec_hbm.1, f32[24,40,1080]{2,1,0:T(8,128)} %adj_hbm.1, f32[24,40]{1,0:T(8,128)} %cx_hbm.1, f32[24,40]{1,0:T(8,128)} %cy_hbm.1, f32[24,40]{1,0:T(8,128)} %wx_hbm.1, f32[24,40]{1,0:T(8,128)} %wy_hbm.1, s32[24,40]{1,0:T(8,128)} %land_hbm.1, s32[24,40]{1,0:T(8,128)} %ice_hbm.1, ...), custom_call_target="tpu_custom_call" | custom-call | tf_op jit(solution)/shard_map/pallas_call | solution.py:625
  24.8 2.1 %copy.14 = f32[24,40,1080]{2,1,0:T(8,128)} copy(f32[24,40,1080]{2,1,0:T(8,128)S(1)} %shard_map.118) | data formatting | bytes 8294400

commit v4 on v3

--- a/solution.py
+++ b/solution.py
@@ -10,8 +10,24 @@
 
 DIRS = 36
 LANES = 128
+LEAST_SPEED = 0.1
+MOST_CURRENT = 0.08
 PAD = 8
 MESH = pl.DeviceIdType.MESH
+
+
+def directions(bins):
+    angles = np.float32(2.0 * math.pi / DIRS) * (np.arange(DIRS, dtype=np.float32) + np.float32(0.5))
+    per_dir = bins // DIRS
+    return np.repeat(np.cos(angles), per_dir), np.repeat(np.sin(angles), per_dir)
+
+
+def one_way(heading):
+    sure = 1.001 * MOST_CURRENT / LEAST_SPEED
+    starts = range(0, heading.size, LANES)
+    forward = [t for t, b in enumerate(starts) if np.all(heading[b : b + LANES] > sure)]
+    backward = [t for t, b in enumerate(starts) if np.all(heading[b : b + LANES] < -sure)]
+    return forward, backward
 
 
 def kernel(
@@ -76,6 +92,18 @@
     has_south = gy > 0
     body = pl.ds(PAD, cols)
 
+    barrier = pltpu.get_barrier_semaphore()
+    for target in (east, west):
+        pl.semaphore_signal(barrier, inc=1, device_id={"gx": target}, device_id_type=MESH)
+
+    @pl.when(has_north)
+    def _():
+        pl.semaphore_signal(barrier, inc=1, device_id={"gy": gy + 1}, device_id_type=MESH)
+
+    @pl.when(has_south)
+    def _():
+        pl.semaphore_signal(barrier, inc=1, device_id={"gy": gy - 1}, device_id_type=MESH)
+
     def local(src, dst, k):
         return pltpu.make_async_copy(src, dst, load_sem.at[k])
 
@@ -118,18 +146,6 @@
     for copy in small + last_row + first_row + col_loads + bulk + ci_loads + [inc_load]:
         copy.start()
 
-    barrier = pltpu.get_barrier_semaphore()
-    for target in (east, west):
-        pl.semaphore_signal(barrier, inc=1, device_id={"gx": target}, device_id_type=MESH)
-
-    @pl.when(has_north)
-    def _():
-        pl.semaphore_signal(barrier, inc=1, device_id={"gy": gy + 1}, device_id_type=MESH)
-
-    @pl.when(has_south)
-    def _():
-        pl.semaphore_signal(barrier, inc=1, device_id={"gy": gy - 1}, device_id_type=MESH)
-
     def remote(src, dst, k, device):
         return pltpu.make_async_remote_copy(
             src_ref=src,
@@ -143,16 +159,37 @@
     to_east, to_west = {"gx": east}, {"gx": west}
     to_north, to_south = {"gy": gy + 1}, {"gy": gy - 1}
 
-    def edge(main, last, lines, k, side):
-        if side == "north":
-            return [remote(lines.at[lines.shape[0] - 2], lines.at[0], k, to_north)]
-        if side == "south":
-            return [remote(lines.at[1], lines.at[lines.shape[0] - 1], k, to_south)]
-        src, dst, device = (rows, 0, to_east) if side == "east" else (1, rows + 1, to_west)
-        return [
-            remote(main.at[src, :, body, :], main.at[dst, :, body, :], k, device),
-            remote(last.at[src, body, :], last.at[dst, body, :], k + 1, device),
-        ]
+    used = iter(range(24))
+
+    def runs(skip):
+        spans, low = [], 0
+        for t in sorted(skip) + [pieces]:
+            if t > low:
+                spans.append((low, t))
+            low = t + 1
+        return spans
+
+    def edge(main, last, lines, side, skip):
+        copies = []
+        for low, high in runs(skip):
+            if side in ("north", "south"):
+                lanes = pl.ds(low * LANES, min(high * LANES, bins) - low * LANES)
+                top = lines.shape[0] - 1
+                src, dst, device = (top - 1, 0, to_north) if side == "north" else (1, top, to_south)
+                copies.append(
+                    remote(lines.at[src, :, lanes], lines.at[dst, :, lanes], next(used), device)
+                )
+                continue
+            src, dst, device = (rows, 0, to_east) if side == "east" else (1, rows + 1, to_west)
+            whole = pl.ds(low, min(high, mains) - low)
+            copies.append(
+                remote(main.at[src, whole, body, :], main.at[dst, whole, body, :], next(used), device)
+            )
+            if high == pieces:
+                copies.append(
+                    remote(last.at[src, body, :], last.at[dst, body, :], next(used), device)
+                )
+        return copies
 
     sides = ("east", "west", "north", "south")
     stat_copies = {}
@@ -160,11 +197,15 @@
         (("east", to_east, 0), ("west", to_west, 0), ("north", to_north, 1), ("south", to_south, 1))
     ):
         stat_copies[side] = [
-            remote(stat_i.at[0], nb_i.at[s], 16 + 2 * s, device),
-            remote(stat_f.at[field], nb_f.at[s], 17 + 2 * s, device),
+            remote(stat_i.at[0], nb_i.at[s], next(used), device),
+            remote(stat_f.at[field], nb_f.at[s], next(used), device),
         ]
-    one = {side: edge(sp_main, sp_tail, col, 2 * s, side) for s, side in enumerate(sides)}
-    two = {side: edge(ss_main, ss_tail, sc, 8 + 2 * s, side) for s, side in enumerate(sides)}
+    cosine, sine = directions(bins)
+    (eastward, westward), (northward, southward) = one_way(cosine), one_way(sine)
+    idle_one = {"east": westward, "west": eastward, "north": southward, "south": northward}
+    idle_two = {"east": eastward, "west": westward, "north": northward, "south": southward}
+    one = {side: edge(sp_main, sp_tail, col, side, idle_one[side]) for side in sides}
+    two = {side: edge(ss_main, ss_tail, sc, side, idle_two[side]) for side in sides}
 
     sends_ok = {"east": None, "west": None, "north": has_north, "south": has_south}
     recvs_ok = {"east": None, "west": None, "north": has_south, "south": has_north}
@@ -207,11 +248,14 @@
         down = jnp.where(has_south, down, 0.0)
         return jnp.where(lane == cols, up, jnp.where(lane == LANES - 1, down, mine))
 
-    def spread(field, places):
-        turned = jnp.transpose(field)
-        for dst, spot, column, r in places:
+    def spread(places):
+        turned = {}
+        for field, dst, spot, column, r in places:
+            if id(field) not in turned:
+                turned[id(field)] = jnp.transpose(field)
+        for field, dst, spot, column, r in sorted(places, key=lambda place: place[4]):
             count = column.stop - column.start
-            dst[spot] = jnp.broadcast_to(turned[column, r : r + 1], (count, LANES))
+            dst[spot] = jnp.broadcast_to(turned[id(field)][column, r : r + 1], (count, LANES))
 
     inside = slice(0, cols)
     inside_at = pl.ds(PAD, cols)
@@ -249,13 +293,17 @@
         sea = widened(sea_of(stat_i[0]))
         wet = widened(sea_of(stat_i[1])) * sea
         every = range(rows)
-        spread(sea, [(seas, r, inside, r) for r in every])
-        spread(widened(stat_f[2]) * wet, [(wxs, r, inside, r) for r in every])
-        spread(widened(stat_f[3]) * wet, [(wys, r, inside, r) for r in every])
-        for field, dst in zip(lon_faces(sea, widened(stat_f[0])), (oxs, pxs)):
-            spread(field, [(dst, r + 1, inside, r) for r in range(rows - 1)])
-        for field, dst in zip(lat_faces(sea, widened(stat_f[1])), (oys, pys)):
-            spread(field, [(dst, (r, inside_at), inside, r) for r in every])
+        lon = lon_faces(sea, widened(stat_f[0]))
+        lat = lat_faces(sea, widened(stat_f[1]))
+        breeze = [widened(stat_f[2]) * wet, widened(stat_f[3]) * wet]
+        places = []
+        for r in every:
+            places += [(field, dst, r, inside, r) for field, dst in zip(breeze + [sea], (wxs, wys, seas))]
+            places += [(field, dst, (r, inside_at), inside, r) for field, dst in zip(lat, (oys, pys))]
+            if r < rows - 1:
+                places += [(field, dst, r + 1, inside, r) for field, dst in zip(lon, (oxs, pxs))]
+        spread(places)
+        for dst in (oys, pys):
             for r in every:
                 dst[r, pl.ds(0, PAD), :] = jnp.zeros((PAD, LANES), jnp.float32)
 
@@ -265,11 +313,13 @@
         sea_lat = around_lat(sea, sea_of(nb_i[3]), sea_of(nb_i[2]))
         drift_lon = around_lon(widened(stat_f[0]), nb_f[1], nb_f[0])
         drift_lat = around_lat(widened(stat_f[1]), nb_f[3], nb_f[2])
-        for field, dst in zip(lon_faces(sea_lon, drift_lon), (oxs, pxs)):
-            spread(field, [(dst, 0, inside, 31), (dst, rows, inside, rows - 1)])
         wet = widened(sea_of(stat_i[1])) * sea
         lon = lon_faces(sea_lon, drift_lon)
         lat = lat_faces(sea_lat, drift_lat)
+        places = []
+        for field, dst in zip(lon, (oxs, pxs)):
+            places += [(field, dst, 0, inside, 31), (field, dst, rows, inside, rows - 1)]
+        spread(places)
         fields = list(lon) + [pltpu.roll(field, 1, 0) for field in lon]
         fields += list(lat) + [pltpu.roll(field, 1, 1) for field in lat]
         fields += [widened(stat_f[2]) * wet, widened(stat_f[3]) * wet, sea]
@@ -313,7 +363,9 @@
         line = PAD + 8 * jt
         pace = oxs[i + 1, spot, :][cut] * table(0, t) + pxs[i + 1, spot, :][cut]
         here, e = at(sp_main, sp_tail, i + 1, t, line), at(sp_main, sp_tail, i + 2, t, line)
-        return pace * jnp.where(pace > 0.0, here, e)
+        if isinstance(i, int) and i < 0:
+            return pace * jnp.where(pace > 0.0, here, e)
+        return pace * jnp.where(pace < 0.0, e, here)
 
     def tally(i, jt, parts):
         whole = parts[0]
@@ -386,11 +438,13 @@
                 value = at(ss_main, ss_tail, i + 1, t, line) - pull[:, : width_of(t)]
                 put(ss_main, ss_tail, i + 1, t, line, value)
 
-    def source(low, count, jts):
+    def source(low, count, jts, before_weigh=None):
         jts = list(jts)
         prime(low, jts)
         spans = [(jts[0], len(jts))] if jts[-1] - jts[0] == len(jts) - 1 else [(jt, 1) for jt in jts]
         for step in (advect, weigh, settle):
+            if step is weigh and before_weigh is not None:
+                before_weigh()
             if count == 1:
                 step(low, jts)
             else:
@@ -504,6 +558,8 @@
         for jt in range(tiles):
             spot = pl.ds(8 * jt, 8)
             for t in range(pieces):
+                if t in (idle_two["east"] if i == 0 else idle_two["west"]):
+                    continue
                 cut = (slice(None), slice(0, width_of(t)))
                 here = at(ss_main, ss_tail, i + 1, t, PAD + 8 * jt)
                 if i == 0:
@@ -542,14 +598,17 @@
     everywhere = range(tiles)
     early = gy == ny // 2
     late = gy != ny // 2
-    first_part = (rows - 2) * 3 // 5
+    from_fold = lax.rem(gy + ny // 2, ny)
+    beside = jnp.logical_or(from_fold < 2, from_fold >= ny - 1)
+    beside = jnp.logical_or(beside, jnp.logical_or(gy == 0, gy == ny - 1))
+    away = jnp.logical_not(beside)
+    first_part = (rows - 2) * 5 // 11
 
     def first_source():
+        prepare()
         for copy in bulk:
             copy.wait()
-        inc_load.wait()
-        prepare()
-        source(1, first_part, everywhere)
+        source(1, first_part, everywhere, inc_load.wait)
 
     def second_source():
         source(1 + first_part, rows - 2 - first_part, everywhere)
@@ -564,7 +623,7 @@
     for side in ("north", "south", "east", "west"):
         start(one, side)
     pl.when(late)(first_source)
-    pl.when(early)(second_source)
+    pl.when(beside)(second_source)
     for copy in col_loads[2:] + ci_loads:
         copy.wait()
     for side in sides:
@@ -580,7 +639,7 @@
     insert_columns((0, rows - 1))
     start(two, "east")
     start(two, "west")
-    pl.when(late)(second_source)
+    pl.when(away)(second_source)
     insert_columns(range(1, rows - 1))
     looped(1, rows - 1, lambda i: transport([(i, jt) for jt in everywhere]))
     transport([(0, jt) for jt in everywhere], skip_w=True)
@@ -613,10 +672,8 @@
 ):
     rows, cols, bins = spectrum.shape
     freqs = group_speed.shape[0]
-    angles = np.float32(2.0 * math.pi / DIRS) * (np.arange(DIRS, dtype=np.float32) + np.float32(0.5))
     wave = np.zeros((8, -(-bins // LANES) * LANES), np.float32)
-    wave[0, :bins] = np.repeat(np.cos(angles), freqs)
-    wave[1, :bins] = np.repeat(np.sin(angles), freqs)
+    wave[0, :bins], wave[1, :bins] = directions(bins)
     mains = bins // LANES
     tail = bins - mains * LANES
     tall = cols + 2 * PAD

time: 27.1 us -> 23.6 us (0.87)
  the two profiles are of different devices: /device:TPU:17 before, /device:TPU:24 now
where the time goes in v4:
time: 23.6 us; the launch traced here: 23.5 us
  Pallas kernels  21.4 us (91%)
  local copies, waits for them, and re-layouts  2.09 us (9%)
    pallas_call x1, Pallas kernels, body(): pl.pallas_call(kernel, out_shape=pltpu.VMEM((rows, cols, bins), f32), in_...  21.4 us
    unnamed x1, local copies, waits for them, and re-layouts  2.09 us

profile of v4, /device:TPU:24, one launch (start us, length us, event | category | flops | bytes accessed | tf_op | source)
XLA Modules:
  0.0 23.5 jit_solution(3410428675442644636)
XLA Ops:
  0.0 21.4 %shard_map.118 = f32[24,40,1080]{2,1,0:T(8,128)S(1)} custom-call(f32[24,40,1080]{2,1,0:T(8,128)} %spec_hbm.1, f32[24,40,1080]{2,1,0:T(8,128)} %adj_hbm.1, f32[24,40]{1,0:T(8,128)} %cx_hbm.1, f32[24,40]{1,0:T(8,128)} %cy_hbm.1, f32[24,40]{1,0:T(8,128)} %wx_hbm.1, f32[24,40]{1,0:T(8,128)} %wy_hbm.1, s32[24,40]{1,0:T(8,128)} %land_hbm.1, s32[24,40]{1,0:T(8,128)} %ice_hbm.1, ...), custom_call_target="tpu_custom_call" | custom-call | tf_op jit(solution)/shard_map/pallas_call | solution.py:682
  21.4 2.1 %copy.14 = f32[24,40,1080]{2,1,0:T(8,128)} copy(f32[24,40,1080]{2,1,0:T(8,128)S(1)} %shard_map.118) | data formatting | bytes 8294400

commit v5 on v4

--- a/solution.py
+++ b/solution.py
@@ -357,14 +357,14 @@
 
     scale = 1.0 / bins
 
-    def lon_flux(i, jt, t):
+    def lon_flux(i, jt, t, from_west=False):
         cut = (slice(None), slice(0, width_of(t)))
         spot = pl.ds(8 * jt, 8)
         line = PAD + 8 * jt
         pace = oxs[i + 1, spot, :][cut] * table(0, t) + pxs[i + 1, spot, :][cut]
         here, e = at(sp_main, sp_tail, i + 1, t, line), at(sp_main, sp_tail, i + 2, t, line)
-        if isinstance(i, int) and i < 0:
-            return pace * jnp.where(pace > 0.0, here, e)
+        if from_west:
+            return jnp.where(pace > 0.0, pace * here, jnp.where(pace < 0.0, pace * e, 0.0))
         return pace * jnp.where(pace < 0.0, e, here)
 
     def tally(i, jt, parts):
@@ -377,7 +377,7 @@
     def prime(i, jts):
         for jt in jts:
             for t in range(pieces):
-                fx[jt, t, :, pl.ds(0, width_of(t))] = lon_flux(i - 1, jt, t)
+                fx[jt, t, :, pl.ds(0, width_of(t))] = lon_flux(i - 1, jt, t, True)
 
     def advect(i, jts):
         for jt in jts:
@@ -472,8 +472,7 @@
     def wide_table(k, t):
         return jnp.broadcast_to(tab[k * pieces + t, pl.ds(0, 1), pl.ds(0, width_of(t))], (rows, width_of(t)))
 
-    def edge_columns():
-        ends = (0, 1)
+    def edge_columns(ends):
         places = (PAD, PAD + cols - 1)
         sums = [[], []]
         for k in ends:
@@ -498,7 +497,7 @@
                 moved = here - lon - lat
                 sc[1 + k, :, lanes_of(t)] = moved
                 sums[k].append(moved)
-        energies = [lane_sum(sums[k]) * scale for k in ends]
+        energies = {k: lane_sum(sums[k]) * scale for k in ends}
         pulls = [[], []]
         for k in ends:
             energy = jnp.broadcast_to(energies[k], (rows, LANES))
@@ -516,7 +515,7 @@
                 weighted = ci[k, :, lanes_of(t)] * gain * inverse
                 sc[1 + k, :, lanes_of(t)] = weighted
                 pulls[k].append(weighted * loss * moved)
-        ends_pull = [lane_sum(pulls[k]) * scale for k in ends]
+        ends_pull = {k: lane_sum(pulls[k]) * scale for k in ends}
         for k in ends:
             pull = jnp.broadcast_to(ends_pull[k], (rows, LANES))
             for t in range(pieces):
@@ -598,10 +597,6 @@
     everywhere = range(tiles)
     early = gy == ny // 2
     late = gy != ny // 2
-    from_fold = lax.rem(gy + ny // 2, ny)
-    beside = jnp.logical_or(from_fold < 2, from_fold >= ny - 1)
-    beside = jnp.logical_or(beside, jnp.logical_or(gy == 0, gy == ny - 1))
-    away = jnp.logical_not(beside)
     first_part = (rows - 2) * 5 // 11
 
     def first_source():
@@ -618,12 +613,14 @@
     pl.when(early)(first_source)
     peers = 2 + lax.div(gy + ny - 1, ny) + lax.div(2 * ny - 2 - gy, ny)
     pl.semaphore_wait(barrier, peers)
-    for side in sides:
+    for side in ("south", "north"):
         start(stat_copies, side)
-    for side in ("north", "south", "east", "west"):
+        start(one, side)
+    for side in ("east", "west"):
+        start(stat_copies, side)
         start(one, side)
     pl.when(late)(first_source)
-    pl.when(beside)(second_source)
+    second_source()
     for copy in col_loads[2:] + ci_loads:
         copy.wait()
     for side in sides:
@@ -631,15 +628,20 @@
     prepare_edges()
     for side in sides:
         wait_recv(one, side)
-    edge_columns()
+    edge_columns((1,))
     start(two, "north")
+    edge_columns((0,))
     start(two, "south")
-    source(rows - 1, 1, everywhere)
-    source(0, 1, everywhere)
-    insert_columns((0, rows - 1))
-    start(two, "east")
-    start(two, "west")
-    pl.when(away)(second_source)
+    odd = lax.rem(gx, 2)
+    for near in (0, 1):
+        source((odd if near == 0 else 1 - odd) * (rows - 1), 1, everywhere)
+        for turn, side, i in ((near, "west", 0), (1 - near, "east", rows - 1)):
+
+            @pl.when(odd == turn)
+            def _(side=side, i=i):
+                insert_columns((i,))
+                start(two, side)
+
     insert_columns(range(1, rows - 1))
     looped(1, rows - 1, lambda i: transport([(i, jt) for jt in everywhere]))
     transport([(0, jt) for jt in everywhere], skip_w=True)

time: 23.6 us -> 23.4 us (level)
  no operation moved by 1% of the time
where the time goes in v5:
time: 23.4 us; the launch traced here: 23.3 us
  Pallas kernels  21.2 us (91%)
  local copies, waits for them, and re-layouts  2.09 us (9%)
    pallas_call x1, Pallas kernels, body(): pl.pallas_call(kernel, out_shape=pltpu.VMEM((rows, cols, bins), f32), in_...  21.2 us
    unnamed x1, local copies, waits for them, and re-layouts  2.09 us

profile of v5, /device:TPU:24, one launch (start us, length us, event | category | flops | bytes accessed | tf_op | source)
XLA Modules:
  0.0 23.3 jit_solution(17419096728011757130)
XLA Ops:
  0.0 21.2 %shard_map.118 = f32[24,40,1080]{2,1,0:T(8,128)S(1)} custom-call(f32[24,40,1080]{2,1,0:T(8,128)} %spec_hbm.1, f32[24,40,1080]{2,1,0:T(8,128)} %adj_hbm.1, f32[24,40]{1,0:T(8,128)} %cx_hbm.1, f32[24,40]{1,0:T(8,128)} %cy_hbm.1, f32[24,40]{1,0:T(8,128)} %wx_hbm.1, f32[24,40]{1,0:T(8,128)} %wy_hbm.1, s32[24,40]{1,0:T(8,128)} %land_hbm.1, s32[24,40]{1,0:T(8,128)} %ice_hbm.1, ...), custom_call_target="tpu_custom_call" | custom-call | tf_op jit(solution)/shard_map/pallas_call | solution.py:684
  21.2 2.1 %copy.14 = f32[24,40,1080]{2,1,0:T(8,128)} copy(f32[24,40,1080]{2,1,0:T(8,128)S(1)} %shard_map.118) | data formatting | bytes 8294400

commit v6 on v5

--- a/solution.py
+++ b/solution.py
@@ -597,7 +597,7 @@
     everywhere = range(tiles)
     early = gy == ny // 2
     late = gy != ny // 2
-    first_part = (rows - 2) * 5 // 11
+    first_part = (rows - 2) * 3 // 11
 
     def first_source():
         prepare()

time: 23.4 us -> 23.4 us (level)
  no operation moved by 1% of the time
where the time goes in v6:
time: 23.4 us; the launch traced here: 23.3 us
  Pallas kernels  21.2 us (91%)
  local copies, waits for them, and re-layouts  2.09 us (9%)
    pallas_call x1, Pallas kernels, body(): pl.pallas_call(kernel, out_shape=pltpu.VMEM((rows, cols, bins), f32), in_...  21.2 us
    unnamed x1, local copies, waits for them, and re-layouts  2.09 us

profile of v6, /device:TPU:24, one launch (start us, length us, event | category | flops | bytes accessed | tf_op | source)
XLA Modules:
  0.0 23.3 jit_solution(1646398960858080815)
XLA Ops:
  0.0 21.2 %shard_map.118 = f32[24,40,1080]{2,1,0:T(8,128)S(1)} custom-call(f32[24,40,1080]{2,1,0:T(8,128)} %spec_hbm.1, f32[24,40,1080]{2,1,0:T(8,128)} %adj_hbm.1, f32[24,40]{1,0:T(8,128)} %cx_hbm.1, f32[24,40]{1,0:T(8,128)} %cy_hbm.1, f32[24,40]{1,0:T(8,128)} %wx_hbm.1, f32[24,40]{1,0:T(8,128)} %wy_hbm.1, s32[24,40]{1,0:T(8,128)} %land_hbm.1, s32[24,40]{1,0:T(8,128)} %ice_hbm.1, ...), custom_call_target="tpu_custom_call" | custom-call | tf_op jit(solution)/shard_map/pallas_call | solution.py:684
  21.2 2.1 %copy.14 = f32[24,40,1080]{2,1,0:T(8,128)} copy(f32[24,40,1080]{2,1,0:T(8,128)S(1)} %shard_map.118) | data formatting | bytes 8294400
